TPU v7x, 32 devices: a 4x2x2 block of a 4x4x8 slice. The times are simulated.
32 devices in a mesh: dp: 4 (over y, z), sp: 8 (over x, core).
Axes of the slice: x: 4, y: 2, z: 2, core: 2. Of those that a mesh axis runs over, the one named last changes fastest.
The devices are a block of a 4x4x8 slice.
Arguments:
- tokens: bfloat16 [131072, 1024], P(('dp', 'sp')), parts along dimension 0
- w_q: bfloat16 [1024, 1024], replicated
- w_k: bfloat16 [1024, 1024], replicated
- w_v: bfloat16 [1024, 1024], replicated
- w_o: bfloat16 [1024, 1024], replicated
- grad_y: bfloat16 [131072, 1024], P(('dp', 'sp')), parts along dimension 0
Outputs:
- output 1: bfloat16 [131072, 1024], P(('dp', 'sp')), parts along dimension 0
- output 2: bfloat16 [131072, 1024], P(('dp', 'sp')), parts along dimension 0
- output 3: float32 [4096, 1024], P('dp'), parts along dimension 0
- output 4: float32 [4096, 1024], P('dp'), parts along dimension 0
- output 5: float32 [4096, 1024], P('dp'), parts along dimension 0
- output 6: float32 [4096, 1024], P('dp'), parts along dimension 0
There are 4 independent parts. A program takes and returns all parts, laid end to end along the dimension named above; an argument that names none is the same for every part.
All inputs are finite; a program needn't handle non-finite values.
Results may differ from a plain program's by a relative error of at most 0.00401916.
Values are sent between devices in bfloat16 or wider.
A program may use at most 768 MiB of HBM per device.

v0:
```python
import math
import jax
import jax.numpy as jnp
from jax import lax
from jax.sharding import PartitionSpec as P

HEAD_DIM = 128
BLOCK_LEN = 128


def solution(mesh):
    n_seq = mesh.shape["sp"]
    fwd_perm = [(j, j + 1) for j in range(n_seq - 1)]
    rev_perm = [(j + 1, j) for j in range(n_seq - 1)]
    row_spec = P(("dp", "sp"), None)
    grad_spec = P("dp", None)

    def local_layer(tokens, w_q, w_k, w_v, w_o, grad_y):
        n_rows, model_dim = tokens.shape
        n_heads = model_dim // HEAD_DIM
        n_blocks = n_rows // BLOCK_LEN
        att_scale = 1.0 / math.sqrt(n_rows * n_seq * HEAD_DIM)
        causal = jnp.arange(BLOCK_LEN)[:, None] >= jnp.arange(BLOCK_LEN)[None, :]

        def project(operand, weight):
            return jnp.dot(operand, weight, preferred_element_type=jnp.float32).astype(jnp.bfloat16)

        def back_proj(rows, weight):
            return jnp.einsum("ne,de->nd", rows, weight, preferred_element_type=jnp.float32)

        def weight_grad(left_rows, right_rows):
            return jnp.einsum("nd,ne->de", left_rows, right_rows, preferred_element_type=jnp.float32)

        def split_heads(tensor):
            return tensor.reshape(n_blocks, BLOCK_LEN, n_heads, HEAD_DIM)

        def to_rows(tensor):
            return (tensor * att_scale).astype(jnp.bfloat16).reshape(n_rows, model_dim)

        q_heads = split_heads(project(tokens, w_q))
        k_heads = split_heads(project(tokens, w_k))
        v_heads = split_heads(project(tokens, w_v))
        block_kv = jnp.einsum("nshd,nshe->nhde", k_heads, v_heads, preferred_element_type=jnp.float32)
        kv_total = jnp.sum(block_kv, axis=0)

        def fwd_hop(hop_index, carried):
            return lax.ppermute(carried + kv_total, "sp", perm=fwd_perm)

        kv_in = lax.fori_loop(0, n_seq - 1, fwd_hop, jnp.zeros_like(kv_total))
        fwd_state = (kv_in + jnp.cumsum(block_kv, axis=0) - block_kv).astype(jnp.bfloat16)
        scores = jnp.einsum("nthd,nshd->nhts", q_heads, k_heads, preferred_element_type=jnp.float32)
        masked_scores = jnp.where(causal, scores, 0.0).astype(jnp.bfloat16)
        out_rows = to_rows(jnp.einsum("nhts,nshe->nthe", masked_scores, v_heads, preferred_element_type=jnp.float32) + jnp.einsum("nthd,nhde->nthe", q_heads, fwd_state, preferred_element_type=jnp.float32))
        out_y = project(out_rows, w_o)

        do_heads = split_heads(back_proj(grad_y, w_o).astype(jnp.bfloat16))
        block_qdo = jnp.einsum("nthd,nthe->nhde", q_heads, do_heads, preferred_element_type=jnp.float32)
        qdo_total = jnp.sum(block_qdo, axis=0)

        def rev_hop(hop_index, carried):
            return lax.ppermute(carried + qdo_total, "sp", perm=rev_perm)

        qdo_in = lax.fori_loop(0, n_seq - 1, rev_hop, jnp.zeros_like(qdo_total))
        rev_state = (qdo_in + qdo_total - jnp.cumsum(block_qdo, axis=0)).astype(jnp.bfloat16)
        d_scores = jnp.einsum("nthe,nshe->nhts", do_heads, v_heads, preferred_element_type=jnp.float32)
        masked_grads = jnp.where(causal, d_scores, 0.0).astype(jnp.bfloat16)
        dq_rows = to_rows(jnp.einsum("nhts,nshd->nthd", masked_grads, k_heads, preferred_element_type=jnp.float32) + jnp.einsum("nthe,nhde->nthd", do_heads, fwd_state, preferred_element_type=jnp.float32))
        dk_rows = to_rows(jnp.einsum("nhts,nthd->nshd", masked_grads, q_heads, preferred_element_type=jnp.float32) + jnp.einsum("nshe,nhde->nshd", v_heads, rev_state, preferred_element_type=jnp.float32))
        dv_rows = to_rows(jnp.einsum("nhts,nthe->nshe", masked_scores, do_heads, preferred_element_type=jnp.float32) + jnp.einsum("nshd,nhde->nshe", k_heads, rev_state, preferred_element_type=jnp.float32))
        grad_x = (back_proj(dq_rows, w_q) + back_proj(dk_rows, w_k) + back_proj(dv_rows, w_v)).astype(jnp.bfloat16)
        grads = lax.psum((weight_grad(tokens, dq_rows), weight_grad(tokens, dk_rows), weight_grad(tokens, dv_rows), weight_grad(out_rows, grad_y)), "sp")
        return (out_y, grad_x) + tuple(grads)

    return jax.shard_map(local_layer, mesh=mesh, in_specs=(row_spec, P(), P(), P(), P(), row_spec), out_specs=(row_spec, row_spec, grad_spec, grad_spec, grad_spec, grad_spec), check_vma=False)
```

profile of v0, /device:TPU:81, one launch (start us, length us, event | category | flops | bytes accessed | tf_op | source)
XLA Modules:
  0.0 828.6 jit_solution(8426304061149542275)
XLA Ops:
  7.3 14.9 %convert_bitcast_fusion.2 = bf16[512,8,8,128]{3,1,2,0:T(8,128)(2,1)} fusion(bf16[4096,1024]{1,0:T(8,128)(2,1)} %param.10, bf16[1024,1024]{1,0:T(8,128)(2,1)} %param.11), kind=kOutput, calls=%fused_computation.31 | convolution fusion | flops 8594128896 | bytes 18874368 | tf_op jit(solution)/shard_map/dot_general | solution.py:26
  22.2 8.9 %copy.61 = bf16[512,8,8,128]{3,2,1,0:T(8,128)(2,1)} copy(bf16[512,8,8,128]{3,1,2,0:T(8,128)(2,1)} %convert_bitcast_fusion.2) | data formatting | bytes 16777216
  31.2 12.4 %copy.46 = bf16[32,128,8,128]{1,3,2,0:T(8,128)(2,1)} copy(bf16[32,128,8,128]{3,2,1,0:T(8,128)(2,1)} %bitcast.109) | data formatting | bytes 16777216 | tf_op jit(solution)/shard_map/reshape | solution.py:35
  43.6 15.0 %convert_bitcast_fusion = bf16[512,8,8,128]{3,1,2,0:T(8,128)(2,1)} fusion(bf16[4096,1024]{1,0:T(8,128)(2,1)} %param.15, bf16[1024,1024]{1,0:T(8,128)(2,1)} %param.14), kind=kOutput, calls=%fused_computation.29 | convolution fusion | flops 8594128896 | bytes 18874368 | tf_op jit(solution)/shard_map/ne,de->nd/dot_general | solution.py:29
  58.6 8.8 %copy.64 = bf16[512,8,8,128]{3,2,1,0:T(8,128)(2,1)} copy(bf16[512,8,8,128]{3,1,2,0:T(8,128)(2,1)} %convert_bitcast_fusion) | data formatting | bytes 16777216
  67.4 12.4 %copy.51 = bf16[32,128,8,128]{1,3,2,0:T(8,128)(2,1)} copy(bf16[32,128,8,128]{3,2,1,0:T(8,128)(2,1)} %bitcast.110) | data formatting | bytes 16777216 | tf_op jit(solution)/shard_map/reshape | solution.py:35
  79.8 14.8 %convert_bitcast_fusion.3 = bf16[512,8,8,128]{3,1,2,0:T(8,128)(2,1)} fusion(bf16[4096,1024]{1,0:T(8,128)(2,1)} %param.10, bf16[1024,1024]{1,0:T(8,128)(2,1)} %param.13), kind=kOutput, calls=%fused_computation.32 | convolution fusion | flops 8594128896 | bytes 18874368 | tf_op jit(solution)/shard_map/dot_general | solution.py:26
  94.6 8.8 %copy.60 = bf16[512,8,8,128]{3,2,1,0:T(8,128)(2,1)} copy(bf16[512,8,8,128]{3,1,2,0:T(8,128)(2,1)} %convert_bitcast_fusion.3) | data formatting | bytes 16777216
  103.4 14.7 %convert_bitcast_fusion.1 = bf16[512,8,8,128]{3,1,2,0:T(8,128)(2,1)} fusion(bf16[4096,1024]{1,0:T(8,128)(2,1)} %param.10, bf16[1024,1024]{1,0:T(8,128)(2,1)S(1)} %copy-done), kind=kOutput, calls=%fused_computation.30 | convolution fusion | flops 8594128896 | bytes 18874368 | tf_op jit(solution)/shard_map/dot_general | solution.py:26
  118.1 8.8 %copy.62 = bf16[512,8,8,128]{3,2,1,0:T(8,128)(2,1)} copy(bf16[512,8,8,128]{3,1,2,0:T(8,128)(2,1)} %convert_bitcast_fusion.1) | data formatting | bytes 16777216
  126.9 12.5 %copy.36 = bf16[32,128,8,128]{1,3,2,0:T(8,128)(2,1)} copy(bf16[32,128,8,128]{3,2,1,0:T(8,128)(2,1)} %bitcast.106) | data formatting | bytes 16777216 | tf_op jit(solution)/shard_map/reshape | solution.py:35
  139.4 17.4 %fusion.54 = (f32[8,128,128]{2,1,0:T(8,128)S(1)}, f32[32,8,128,128]{3,2,1,0:T(8,128)}) fusion(bf16[32,128,8,128]{1,3,2,0:T(8,128)(2,1)} %copy.46, bf16[32,128,8,128]{1,3,2,0:T(8,128)(2,1)} %copy.51), kind=kOutput, calls=%fused_computation.56 | convolution fusion | flops 1077805056 | bytes 34078720 | tf_op jit(solution)/shard_map/nthd,nthe->nhde/dot_general | solution.py:57
  156.8 11.6 %select_convert_fusion.1 = bf16[32,8,128,128]{3,2,1,0:T(8,128)(2,1)} fusion(pred[128,128]{1,0:T(8,128)(4,1)S(1)} %iota_compare_fusion, bf16[32,128,8,128]{1,3,2,0:T(8,128)(2,1)} %copy.46, bf16[32,128,8,128]{3,2,1,0:T(8,128)(2,1)} %bitcast.107), kind=kOutput, calls=%fused_computation.8 | convolution fusion | flops 1082130432 | bytes 25182208 | tf_op jit(solution)/shard_map/nthd,nshd->nhts/dot_general | solution.py:51
  168.5 12.0 %select_convert_fusion = bf16[32,8,128,128]{3,2,1,0:T(8,128)(2,1)} fusion(pred[128,128]{1,0:T(8,128)(4,1)S(1)} %iota_compare_fusion, bf16[32,128,8,128]{1,3,2,0:T(8,128)(2,1)} %copy.51, bf16[32,128,8,128]{3,2,1,0:T(8,128)(2,1)} %bitcast.102), kind=kOutput, calls=%fused_computation.5 | convolution fusion | flops 1082130432 | bytes 25182208 | tf_op jit(solution)/shard_map/nthe,nshe->nhts/dot_general | solution.py:65
  180.5 13.9 %fusion.57 = f32[32,8,128,128]{3,2,1,0:T(8,128)} fusion(bf16[32,128,8,128]{1,3,2,0:T(8,128)(2,1)} %copy.46, bf16[32,8,128,128]{3,2,1,0:T(8,128)(2,1)} %select_convert_fusion), kind=kOutput, calls=%fused_computation.59 | convolution fusion | flops 1073741824 | bytes 33554432 | tf_op jit(solution)/shard_map/nhts,nthd->nshd/dot_general | solution.py:68
  194.4 14.7 %fusion.53 = (f32[8,128,128]{2,1,0:T(8,128)}, f32[32,8,128,128]{3,2,1,0:T(8,128)}) fusion(bf16[32,128,8,128]{1,3,2,0:T(8,128)(2,1)} %copy.36, bf16[32,128,8,128]{3,2,1,0:T(8,128)(2,1)} %bitcast.103), kind=kOutput, calls=%fused_computation.55 | convolution fusion | flops 1077805056 | bytes 34078720 | tf_op jit(solution)/shard_map/nshd,nshe->nhde/dot_general | solution.py:43
  209.1 17.4 %fusion.56 = f32[32,8,128,128]{3,2,1,0:T(8,128)} fusion(bf16[32,128,8,128]{1,3,2,0:T(8,128)(2,1)} %copy.36, bf16[32,8,128,128]{3,2,1,0:T(8,128)(2,1)} %select_convert_fusion), kind=kOutput, calls=%fused_computation.58 | convolution fusion | flops 1073741824 | bytes 33554432 | tf_op jit(solution)/shard_map/nhts,nshd->nthd/dot_general | solution.py:67
  226.5 13.9 %fusion.58 = f32[32,8,128,128]{3,2,1,0:T(8,128)} fusion(bf16[32,128,8,128]{1,3,2,0:T(8,128)(2,1)} %copy.51, bf16[32,8,128,128]{3,2,1,0:T(8,128)(2,1)} %select_convert_fusion.1), kind=kOutput, calls=%fused_computation.60 | convolution fusion | flops 1073741824 | bytes 33554432 | tf_op jit(solution)/shard_map/nhts,nthe->nshe/dot_general | solution.py:69
  240.4 13.0 %fusion.38 = f32[32,8,128,128]{3,2,1,0:T(8,128)} fusion(bf16[32,8,128,128]{3,2,1,0:T(8,128)(2,1)} %select_convert_fusion.1, bf16[32,128,8,128]{3,2,1,0:T(8,128)(2,1)} %bitcast.104), kind=kOutput, calls=%fused_computation.45 | convolution fusion | flops 1073741824 | bytes 33554432 | tf_op jit(solution)/shard_map/nhts,nshe->nthe/dot_general | solution.py:53
  253.5 80.5 %while.21 = (s32[]{:T(128)}, f32[8,128,128]{2,1,0:T(8,128)S(1)}, f32[8,128,128]{2,1,0:T(8,128)S(1)}, s32[]{:T(128)}) while((s32[]{:T(128)}, f32[8,128,128]{2,1,0:T(8,128)S(1)}, f32[8,128,128]{2,1,0:T(8,128)S(1)}, s32[]{:T(128)}) %tuple.42), condition=%wide.region_6.7_spmd, body=%wide.region_5.6_spmd.sunk | while | flops 131074 | bytes 3670109 | solution.py:63
  258.3 7.5 collective-permute-done.1
  268.6 8.6 %collective-permute-done.1 = f32[8,128,128]{2,1,0:T(8,128)S(1)} collective-permute-done((f32[8,128,128]{2,1,0:T(8,128)}, f32[8,128,128]{2,1,0:T(8,128)S(1)}, u32[]{:S(2)}, u32[]{:S(2)}) %collective-permute-start.1) | collective-permute-done | bytes 524320 | tf_op jit(solution)/shard_map/while/body/eval_jaxpr/ppermute | solution.py:61
  279.9 8.6 %collective-permute-done.1 = f32[8,128,128]{2,1,0:T(8,128)S(1)} collective-permute-done((f32[8,128,128]{2,1,0:T(8,128)}, f32[8,128,128]{2,1,0:T(8,128)S(1)}, u32[]{:S(2)}, u32[]{:S(2)}) %collective-permute-start.1) | collective-permute-done | bytes 524320 | tf_op jit(solution)/shard_map/while/body/eval_jaxpr/ppermute | solution.py:61
  291.3 8.6 %collective-permute-done.1 = f32[8,128,128]{2,1,0:T(8,128)S(1)} collective-permute-done((f32[8,128,128]{2,1,0:T(8,128)}, f32[8,128,128]{2,1,0:T(8,128)S(1)}, u32[]{:S(2)}, u32[]{:S(2)}) %collective-permute-start.1) | collective-permute-done | bytes 524320 | tf_op jit(solution)/shard_map/while/body/eval_jaxpr/ppermute | solution.py:61
  302.7 8.6 %collective-permute-done.1 = f32[8,128,128]{2,1,0:T(8,128)S(1)} collective-permute-done((f32[8,128,128]{2,1,0:T(8,128)}, f32[8,128,128]{2,1,0:T(8,128)S(1)}, u32[]{:S(2)}, u32[]{:S(2)}) %collective-permute-start.1) | collective-permute-done | bytes 524320 | tf_op jit(solution)/shard_map/while/body/eval_jaxpr/ppermute | solution.py:61
  314.0 8.6 %collective-permute-done.1 = f32[8,128,128]{2,1,0:T(8,128)S(1)} collective-permute-done((f32[8,128,128]{2,1,0:T(8,128)}, f32[8,128,128]{2,1,0:T(8,128)S(1)}, u32[]{:S(2)}, u32[]{:S(2)}) %collective-permute-start.1) | collective-permute-done | bytes 524320 | tf_op jit(solution)/shard_map/while/body/eval_jaxpr/ppermute | solution.py:61
  325.4 8.6 %collective-permute-done.1 = f32[8,128,128]{2,1,0:T(8,128)S(1)} collective-permute-done((f32[8,128,128]{2,1,0:T(8,128)}, f32[8,128,128]{2,1,0:T(8,128)S(1)}, u32[]{:S(2)}, u32[]{:S(2)}) %collective-permute-start.1) | collective-permute-done | bytes 524320 | tf_op jit(solution)/shard_map/while/body/eval_jaxpr/ppermute | solution.py:61
  334.1 14.5 %fusion.55 = f32[32,8,128,128]{3,2,1,0:T(8,128)} fusion(f32[32,8,128,128]{3,2,1,0:T(8,128)} %get-tuple-element.73), kind=kOutput, calls=%fused_computation.57 | output fusion | flops 130023424 | bytes 33554432 | tf_op jit(solution)/shard_map/jit(cumsum)/reduce_window_sum | solution.py:64
  348.6 18.8 %fusion.2 = bf16[32,128,8,128]{1,3,2,0:T(8,128)(2,1)} fusion(f32[32,8,128,128]{3,2,1,0:T(8,128)} %fusion.57, bf16[32,128,8,128]{3,2,1,0:T(8,128)(2,1)} %bitcast.105, f32[32,8,128,128]{3,2,1,0:T(8,128)} %fusion.55, f32[8,128,128]{2,1,0:T(8,128)S(1)} %add.57), kind=kOutput, calls=%fused_computation.11 | convolution fusion | flops 1094713344 | bytes 50855936 | tf_op jit(solution)/shard_map/nshe,nhde->nshd/dot_general | solution.py:68
  367.4 12.4 %copy.50 = bf16[32,128,8,128]{3,2,1,0:T(8,128)(2,1)} copy(bf16[32,128,8,128]{1,3,2,0:T(8,128)(2,1)} %fusion.2) | data formatting | bytes 16777216 | tf_op jit(solution)/shard_map/convert_element_type | solution.py:38
  379.8 15.1 %fusion.47 = f32[1024,1024]{0,1:T(8,128)} fusion(bf16[4096,1024]{1,0:T(8,128)(2,1)} %param.10, bf16[512,8,8,128]{3,2,1,0:T(8,128)(2,1)} %bitcast.111), kind=kOutput, calls=%fused_computation.52 | convolution fusion | flops 8589934592 | bytes 20971520 | tf_op jit(solution)/shard_map/nd,ne->de/dot_general | solution.py:32
  394.9 19.0 %fusion.3 = bf16[32,128,8,128]{1,3,2,0:T(8,128)(2,1)} fusion(f32[32,8,128,128]{3,2,1,0:T(8,128)} %fusion.58, bf16[32,128,8,128]{3,2,1,0:T(8,128)(2,1)} %bitcast.108, f32[32,8,128,128]{3,2,1,0:T(8,128)} %fusion.55, f32[8,128,128]{2,1,0:T(8,128)S(1)} %copy-done.3), kind=kOutput, calls=%fused_computation.12 | convolution fusion | flops 1094713344 | bytes 50855936 | tf_op jit(solution)/shard_map/nshd,nhde->nshe/dot_general | solution.py:69
  413.8 12.4 %copy.54 = bf16[32,128,8,128]{3,2,1,0:T(8,128)(2,1)} copy(bf16[32,128,8,128]{1,3,2,0:T(8,128)(2,1)} %fusion.3) | data formatting | bytes 16777216 | tf_op jit(solution)/shard_map/convert_element_type | solution.py:38
  426.2 15.1 %fusion.50 = f32[1024,1024]{0,1:T(8,128)} fusion(bf16[4096,1024]{1,0:T(8,128)(2,1)} %param.10, bf16[512,8,8,128]{3,2,1,0:T(8,128)(2,1)} %bitcast.113), kind=kOutput, calls=%fused_computation.53 | convolution fusion | flops 8589934592 | bytes 20971520 | tf_op jit(solution)/shard_map/nd,ne->de/dot_general | solution.py:32
  441.3 77.1 %while.20 = (s32[]{:T(128)}, f32[8,128,128]{2,1,0:T(8,128)S(1)}, f32[8,128,128]{2,1,0:T(8,128)S(1)}, s32[]{:T(128)}) while((s32[]{:T(128)}, f32[8,128,128]{2,1,0:T(8,128)S(1)}, f32[8,128,128]{2,1,0:T(8,128)S(1)}, s32[]{:T(128)}) %tuple.49), condition=%wide.region_2.0_spmd, body=%wide.region_1.0_spmd.sunk | while | flops 131074 | bytes 3670109 | solution.py:49
  444.1 6.1 collective-permute-done
  518.4 15.1 %subtract_convert_fusion.1 = bf16[32,8,128,128]{3,2,1,0:T(8,128)(2,1)} fusion(f32[32,8,128,128]{3,2,1,0:T(8,128)} %get-tuple-element.71, f32[8,128,128]{2,1,0:T(8,128)S(1)} %get-tuple-element.40), kind=kOutput, calls=%fused_computation.7 | output fusion | flops 142606336 | bytes 25690112 | tf_op jit(solution)/shard_map/jit(cumsum)/reduce_window_sum | solution.py:50
  533.6 15.7 %fusion.1 = bf16[32,128,8,128]{1,3,2,0:T(8,128)(2,1)} fusion(f32[32,8,128,128]{3,2,1,0:T(8,128)} %fusion.56, bf16[32,8,128,128]{3,2,1,0:T(8,128)(2,1)} %subtract_convert_fusion.1, bf16[32,128,8,128]{1,3,2,0:T(8,128)(2,1)} %copy.51), kind=kOutput, calls=%fused_computation.10 | convolution fusion | flops 1086324736 | bytes 41943040 | tf_op jit(solution)/shard_map/nthe,nhde->nthd/dot_general | solution.py:67
  549.2 12.4 %copy.45 = bf16[32,128,8,128]{3,2,1,0:T(8,128)(2,1)} copy(bf16[32,128,8,128]{1,3,2,0:T(8,128)(2,1)} %fusion.1) | data formatting | bytes 16777216 | tf_op jit(solution)/shard_map/convert_element_type | solution.py:38
  561.6 15.4 %fusion.44 = f32[1024,1024]{0,1:T(8,128)} fusion(bf16[4096,1024]{1,0:T(8,128)(2,1)} %param.10, bf16[512,8,8,128]{3,2,1,0:T(8,128)(2,1)} %bitcast.115), kind=kOutput, calls=%fused_computation.51 | convolution fusion | flops 8589934592 | bytes 20971520 | tf_op jit(solution)/shard_map/nd,ne->de/dot_general | solution.py:32
  577.0 15.9 %fusion = bf16[32,128,8,128]{1,3,2,0:T(8,128)(2,1)} fusion(f32[32,8,128,128]{3,2,1,0:T(8,128)} %fusion.38, bf16[32,8,128,128]{3,2,1,0:T(8,128)(2,1)} %subtract_convert_fusion.1, bf16[32,128,8,128]{1,3,2,0:T(8,128)(2,1)} %copy.46), kind=kOutput, calls=%fused_computation.9 | convolution fusion | flops 1086324736 | bytes 41943040 | tf_op jit(solution)/shard_map/nthd,nhde->nthe/dot_general | solution.py:53
  592.9 12.4 %copy.40 = bf16[32,128,8,128]{3,2,1,0:T(8,128)(2,1)} copy(bf16[32,128,8,128]{1,3,2,0:T(8,128)(2,1)} %fusion) | data formatting | bytes 16777216 | tf_op jit(solution)/shard_map/convert_element_type | solution.py:38
  605.3 15.0 %fusion.16 = f32[1024,1024]{1,0:T(8,128)} fusion(bf16[4096,1024]{1,0:T(8,128)(2,1)} %param.15, bf16[512,8,8,128]{3,2,1,0:T(8,128)(2,1)} %bitcast.117), kind=kOutput, calls=%fused_computation.25 | convolution fusion | flops 8589934592 | bytes 20971520 | tf_op jit(solution)/shard_map/nd,ne->de/dot_general | solution.py:32
  620.4 14.9 %fusion.10 = f32[4096,1024]{1,0:T(8,128)} fusion(bf16[1024,1024]{1,0:T(8,128)(2,1)S(1)} %copy-done, bf16[512,8,8,128]{3,2,1,0:T(8,128)(2,1)} %bitcast.112), kind=kOutput, calls=%fused_computation.19 | convolution fusion | flops 8589934592 | bytes 27262976 | tf_op jit(solution)/shard_map/ne,de->nd/dot_general | solution.py:29
  635.3 14.8 %fusion.6 = f32[4096,1024]{1,0:T(8,128)} fusion(bf16[1024,1024]{1,0:T(8,128)(2,1)S(1)} %copy-done.4, bf16[512,8,8,128]{3,2,1,0:T(8,128)(2,1)} %bitcast.114), kind=kOutput, calls=%fused_computation.15 | convolution fusion | flops 8589934592 | bytes 27262976 | tf_op jit(solution)/shard_map/ne,de->nd/dot_general | solution.py:29
  650.1 11.1 %fusion.20 = bf16[4096,1024]{1,0:T(8,128)(2,1)} fusion(bf16[1024,1024]{1,0:T(8,128)(2,1)S(1)} %copy-done.5, bf16[512,8,8,128]{3,2,1,0:T(8,128)(2,1)S(1)} %bitcast.120), kind=kOutput, calls=%fused_computation.33 | convolution fusion | flops 8594128896 | bytes 18874368 | tf_op jit(solution)/shard_map/dot_general | solution.py:26
  661.2 19.8 %add_convert_fusion = bf16[4096,1024]{1,0:T(8,128)(2,1)} fusion(f32[4096,1024]{1,0:T(8,128)} %fusion.6, f32[4096,1024]{1,0:T(8,128)} %fusion.10, bf16[1024,1024]{1,0:T(8,128)(2,1)S(1)} %copy-done.6, bf16[512,8,8,128]{3,2,1,0:T(8,128)(2,1)} %bitcast.116), kind=kOutput, calls=%fused_computation | convolution fusion | flops 8602517504 | bytes 52428800 | tf_op jit(solution)/shard_map/ne,de->nd/dot_general | solution.py:29
  681.0 119.7 %all-reduce.3.cloned.1.call-done = (f32[1024,1024]{0,1:T(8,128)}, f32[1024,1024]{0,1:T(8,128)}, f32[1024,1024]{0,1:T(8,128)}, f32[1024,1024]{1,0:T(8,128)}) async-done(((f32[1024,1024]{0,1:T(8,128)}, f32[1024,1024]{0,1:T(8,128)}, f32[1024,1024]{0,1:T(8,128)}, f32[1024,1024]{1,0:T(8,128)}), (f32[1024,1024]{0,1:T(8,128)}, f32[1024,1024]{0,1:T(8,128)}, f32[1024,1024]{0,1:T(8,128)}, ...) | async-done | bytes 16777232 | tf_op jit(solution)/shard_map/psum | solution.py:71
  (63 shorter events, 113.6 us)
Async XLA Ops:
  7.2 96.3 %copy-start = (bf16[1024,1024]{1,0:T(8,128)(2,1)S(1)}, bf16[1024,1024]{1,0:T(8,128)(2,1)}, u32[]{:S(2)}) copy-start(bf16[1024,1024]{1,0:T(8,128)(2,1)} %param.12) | copy-start | bytes 6291460
  7.2 793.5 %all-reduce.3.cloned.1.call-start = ((), (), s32[]{:S(2)}) async-start(), calls=%async_computation | async-start | bytes 33554432 | tf_op jit(solution)/shard_map/psum | solution.py:71
  254.3 11.5 %collective-permute-start.1 = (f32[8,128,128]{2,1,0:T(8,128)}, f32[8,128,128]{2,1,0:T(8,128)S(1)}, u32[]{:S(2)}, u32[]{:S(2)}) collective-permute-start(f32[8,128,128]{2,1,0:T(8,128)} %add.85), channel_id=1, source_target_pairs={{1,0},{2,1},{3,2},{4,3},{5,4},{6,5},{7,6},{9,8},{10,9},{11,10},{12... | collective-permute-start | bytes 1572872 | tf_op jit(solution)/shard_map/while/body/eval_jaxpr/ppermute | solution.py:61
  266.6 10.5 %collective-permute-start.1 = (f32[8,128,128]{2,1,0:T(8,128)}, f32[8,128,128]{2,1,0:T(8,128)S(1)}, u32[]{:S(2)}, u32[]{:S(2)}) collective-permute-start(f32[8,128,128]{2,1,0:T(8,128)} %add.85), channel_id=1, source_target_pairs={{1,0},{2,1},{3,2},{4,3},{5,4},{6,5},{7,6},{9,8},{10,9},{11,10},{12... | collective-permute-start | bytes 1572872 | tf_op jit(solution)/shard_map/while/body/eval_jaxpr/ppermute | solution.py:61
  278.0 10.5 %collective-permute-start.1 = (f32[8,128,128]{2,1,0:T(8,128)}, f32[8,128,128]{2,1,0:T(8,128)S(1)}, u32[]{:S(2)}, u32[]{:S(2)}) collective-permute-start(f32[8,128,128]{2,1,0:T(8,128)} %add.85), channel_id=1, source_target_pairs={{1,0},{2,1},{3,2},{4,3},{5,4},{6,5},{7,6},{9,8},{10,9},{11,10},{12... | collective-permute-start | bytes 1572872 | tf_op jit(solution)/shard_map/while/body/eval_jaxpr/ppermute | solution.py:61
  289.4 10.5 %collective-permute-start.1 = (f32[8,128,128]{2,1,0:T(8,128)}, f32[8,128,128]{2,1,0:T(8,128)S(1)}, u32[]{:S(2)}, u32[]{:S(2)}) collective-permute-start(f32[8,128,128]{2,1,0:T(8,128)} %add.85), channel_id=1, source_target_pairs={{1,0},{2,1},{3,2},{4,3},{5,4},{6,5},{7,6},{9,8},{10,9},{11,10},{12... | collective-permute-start | bytes 1572872 | tf_op jit(solution)/shard_map/while/body/eval_jaxpr/ppermute | solution.py:61
  300.7 10.5 %collective-permute-start.1 = (f32[8,128,128]{2,1,0:T(8,128)}, f32[8,128,128]{2,1,0:T(8,128)S(1)}, u32[]{:S(2)}, u32[]{:S(2)}) collective-permute-start(f32[8,128,128]{2,1,0:T(8,128)} %add.85), channel_id=1, source_target_pairs={{1,0},{2,1},{3,2},{4,3},{5,4},{6,5},{7,6},{9,8},{10,9},{11,10},{12... | collective-permute-start | bytes 1572872 | tf_op jit(solution)/shard_map/while/body/eval_jaxpr/ppermute | solution.py:61
  312.1 10.5 %collective-permute-start.1 = (f32[8,128,128]{2,1,0:T(8,128)}, f32[8,128,128]{2,1,0:T(8,128)S(1)}, u32[]{:S(2)}, u32[]{:S(2)}) collective-permute-start(f32[8,128,128]{2,1,0:T(8,128)} %add.85), channel_id=1, source_target_pairs={{1,0},{2,1},{3,2},{4,3},{5,4},{6,5},{7,6},{9,8},{10,9},{11,10},{12... | collective-permute-start | bytes 1572872 | tf_op jit(solution)/shard_map/while/body/eval_jaxpr/ppermute | solution.py:61
  323.5 10.5 %collective-permute-start.1 = (f32[8,128,128]{2,1,0:T(8,128)}, f32[8,128,128]{2,1,0:T(8,128)S(1)}, u32[]{:S(2)}, u32[]{:S(2)}) collective-permute-start(f32[8,128,128]{2,1,0:T(8,128)} %add.85), channel_id=1, source_target_pairs={{1,0},{2,1},{3,2},{4,3},{5,4},{6,5},{7,6},{9,8},{10,9},{11,10},{12... | collective-permute-start | bytes 1572872 | tf_op jit(solution)/shard_map/while/body/eval_jaxpr/ppermute | solution.py:61
  334.0 14.5 %copy-start.2 = (f32[8,128,128]{2,1,0:T(8,128)}, f32[8,128,128]{2,1,0:T(8,128)S(1)}, u32[]{:S(2)}) copy-start(f32[8,128,128]{2,1,0:T(8,128)S(1)} %add.57) | copy-start | bytes 1572868
  379.8 15.1 %copy-start.3 = (f32[8,128,128]{2,1,0:T(8,128)S(1)}, f32[8,128,128]{2,1,0:T(8,128)}, u32[]{:S(2)}) copy-start(f32[8,128,128]{2,1,0:T(8,128)} %copy-done.2) | copy-start | bytes 1572868
  426.2 15.1 %copy-start.1 = (f32[8,128,128]{2,1,0:T(8,128)S(1)}, f32[8,128,128]{2,1,0:T(8,128)}, u32[]{:S(2)}) copy-start(f32[8,128,128]{2,1,0:T(8,128)} %get-tuple-element.114) | copy-start | bytes 1572868
  442.2 8.0 collective-permute-start
  451.1 10.5 %collective-permute-start = (f32[8,128,128]{2,1,0:T(8,128)}, f32[8,128,128]{2,1,0:T(8,128)S(1)}, u32[]{:S(2)}, u32[]{:S(2)}) collective-permute-start(f32[8,128,128]{2,1,0:T(8,128)} %add.83), channel_id=1, source_target_pairs={{0,1},{1,2},{2,3},{3,4},{4,5},{5,6},{6,7},{8,9},{9,10},{10,11},{11... | collective-permute-start | bytes 1572872 | tf_op jit(solution)/shard_map/while/body/eval_jaxpr/ppermute | solution.py:47
  462.4 10.5 %collective-permute-start = (f32[8,128,128]{2,1,0:T(8,128)}, f32[8,128,128]{2,1,0:T(8,128)S(1)}, u32[]{:S(2)}, u32[]{:S(2)}) collective-permute-start(f32[8,128,128]{2,1,0:T(8,128)} %add.83), channel_id=1, source_target_pairs={{0,1},{1,2},{2,3},{3,4},{4,5},{5,6},{6,7},{8,9},{9,10},{10,11},{11... | collective-permute-start | bytes 1572872 | tf_op jit(solution)/shard_map/while/body/eval_jaxpr/ppermute | solution.py:47
  473.8 10.5 %collective-permute-start = (f32[8,128,128]{2,1,0:T(8,128)}, f32[8,128,128]{2,1,0:T(8,128)S(1)}, u32[]{:S(2)}, u32[]{:S(2)}) collective-permute-start(f32[8,128,128]{2,1,0:T(8,128)} %add.83), channel_id=1, source_target_pairs={{0,1},{1,2},{2,3},{3,4},{4,5},{5,6},{6,7},{8,9},{9,10},{10,11},{11... | collective-permute-start | bytes 1572872 | tf_op jit(solution)/shard_map/while/body/eval_jaxpr/ppermute | solution.py:47
  485.2 10.5 %collective-permute-start = (f32[8,128,128]{2,1,0:T(8,128)}, f32[8,128,128]{2,1,0:T(8,128)S(1)}, u32[]{:S(2)}, u32[]{:S(2)}) collective-permute-start(f32[8,128,128]{2,1,0:T(8,128)} %add.83), channel_id=1, source_target_pairs={{0,1},{1,2},{2,3},{3,4},{4,5},{5,6},{6,7},{8,9},{9,10},{10,11},{11... | collective-permute-start | bytes 1572872 | tf_op jit(solution)/shard_map/while/body/eval_jaxpr/ppermute | solution.py:47
  496.5 10.5 %collective-permute-start = (f32[8,128,128]{2,1,0:T(8,128)}, f32[8,128,128]{2,1,0:T(8,128)S(1)}, u32[]{:S(2)}, u32[]{:S(2)}) collective-permute-start(f32[8,128,128]{2,1,0:T(8,128)} %add.83), channel_id=1, source_target_pairs={{0,1},{1,2},{2,3},{3,4},{4,5},{5,6},{6,7},{8,9},{9,10},{10,11},{11... | collective-permute-start | bytes 1572872 | tf_op jit(solution)/shard_map/while/body/eval_jaxpr/ppermute | solution.py:47
  507.9 10.5 %collective-permute-start = (f32[8,128,128]{2,1,0:T(8,128)}, f32[8,128,128]{2,1,0:T(8,128)S(1)}, u32[]{:S(2)}, u32[]{:S(2)}) collective-permute-start(f32[8,128,128]{2,1,0:T(8,128)} %add.83), channel_id=1, source_target_pairs={{0,1},{1,2},{2,3},{3,4},{4,5},{5,6},{6,7},{8,9},{9,10},{10,11},{11... | collective-permute-start | bytes 1572872 | tf_op jit(solution)/shard_map/while/body/eval_jaxpr/ppermute | solution.py:47
  620.4 14.9 %copy-start.4 = (bf16[1024,1024]{1,0:T(8,128)(2,1)S(1)}, bf16[1024,1024]{1,0:T(8,128)(2,1)}, u32[]{:S(2)}) copy-start(bf16[1024,1024]{1,0:T(8,128)(2,1)} %param.13) | copy-start | bytes 6291460
  620.4 29.7 %slice-start = ((s8[8388608]{0:T(1024)(128)(4,1)}), s8[4194304]{0:T(1024)(128)(4,1)S(1)}, s32[]{:S(2)}) async-start(s8[8388608]{0:T(1024)(128)(4,1)} %bitcast.118), calls=%async_computation.1 | async-start | bytes 8388608
  635.3 14.8 %slice-start.1 = ((s8[8388608]{0:T(1024)(128)(4,1)}), s8[4194304]{0:T(1024)(128)(4,1)S(1)}, s32[]{:S(2)}) async-start(s8[8388608]{0:T(1024)(128)(4,1)} %bitcast.118), calls=%async_computation.2 | async-start | bytes 8388608
  635.3 14.8 %copy-start.5 = (bf16[1024,1024]{1,0:T(8,128)(2,1)S(1)}, bf16[1024,1024]{1,0:T(8,128)(2,1)}, u32[]{:S(2)}) copy-start(bf16[1024,1024]{1,0:T(8,128)(2,1)} %param.14) | copy-start | bytes 6291460
  650.1 11.1 %copy-start.6 = (bf16[1024,1024]{1,0:T(8,128)(2,1)S(1)}, bf16[1024,1024]{1,0:T(8,128)(2,1)}, u32[]{:S(2)}) copy-start(bf16[1024,1024]{1,0:T(8,128)(2,1)} %param.11) | copy-start | bytes 6291460
Sparse Core Ops, SparseCore 0:
  620.5 180.1 all-reduce.2
where the time goes:
time: 840 us; the launch traced here: 829 us
  matrix products  364 us (43%)
  waiting for transfers between devices  221 us (26%)
  local copies, waits for them, and re-layouts  143 us (17%)
  starting transfers between devices  44.2 us (5%)
  other arithmetic  41.6 us (5%)
  between operations  14.4 us (2%)
    psum x1, waiting for transfers between devices, local_layer(): lax.psum((weight_grad(tokens, dq_rows), weight_grad(tokens, dk_rows), wei...  120 us
    dot_general x4, matrix products, back_proj(): jnp.einsum('ne,de->nd', rows, weight, preferred_element_type=jnp.float32)  64.5 us
    dot_general x4, matrix products, weight_grad(): jnp.einsum('nd,ne->de', left_rows, right_rows, preferred_element_type=jnp...  60.6 us
    ppermute x7, waiting for transfers between devices, rev_hop(): return lax.ppermute(carried + qdo_total, 'sp', perm=rev_perm)  58.9 us
    unnamed x26, local copies, waits for them, and re-layouts  56.1 us
    dot_general x4, matrix products, project(): jnp.dot(operand, weight, preferred_element_type=jnp.float32)  55.5 us
    convert_element_type x4, local copies, waits for them, and re-layouts, to_rows(): return (tensor * att_scale).astype(jnp.bfloat16).reshape(n_rows, model_dim)  49.5 us
    ppermute x7, waiting for transfers between devices, fwd_hop(): return lax.ppermute(carried + kv_total, 'sp', perm=fwd_perm)  42.6 us
  transfers between devices with their start and end apart: 15, of which 15 were waited for; matrix products, arithmetic and copies ran while one was open for 7% of the time, Pallas kernels for 0%

commit v1 on v0

v1 whole, which is shorter than its diff:
```python
import functools
import math
import jax
import jax.numpy as jnp
from jax import lax
from jax.experimental import pallas as pl
from jax.experimental.pallas import tpu as pltpu
from jax.sharding import PartitionSpec as P

HEAD_DIM = 128
BLOCK_LEN = 128
BF16 = jnp.bfloat16
F32 = jnp.float32
MESH = pl.DeviceIdType.MESH
VMEM_LIMIT = 64 * 1024 * 1024 - 1024 * 64


def dot(a, b):
    return lax.dot_general(a, b, (((1,), (0,)), ((), ())), preferred_element_type=F32)


def dot_nt(a, b):
    return lax.dot_general(a, b, (((1,), (1,)), ((), ())), preferred_element_type=F32)


def dot_tn(a, b):
    return lax.dot_general(a, b, (((0,), (0,)), ((), ())), preferred_element_type=F32)


def project_kernel(x_ref, dy_ref, wq_ref, wk_ref, wv_ref, wo_ref, q_ref, k_ref, v_ref, do_ref, tot_ref):
    @pl.when(pl.program_id(0) == 0)
    def _():
        tot_ref[...] = jnp.zeros_like(tot_ref)

    x = x_ref[...]
    q_ref[...] = dot(x, wq_ref[...]).astype(BF16)
    k_ref[...] = dot(x, wk_ref[...]).astype(BF16)
    v_ref[...] = dot(x, wv_ref[...]).astype(BF16)
    do_ref[...] = dot_nt(dy_ref[...], wo_ref[...]).astype(BF16)
    n_heads = x.shape[1] // HEAD_DIM
    for h in range(n_heads):
        cols = slice(h * HEAD_DIM, (h + 1) * HEAD_DIM)
        tot_ref[0, h] += dot_tn(k_ref[:, cols], v_ref[:, cols])
        tot_ref[1, h] += dot_tn(q_ref[:, cols], do_ref[:, cols])


def exchange_kernel(n_chips, tot_ref, init_ref, part, chip, recv, half, d2d_sem, send_sem, recv_sem, half_sem):
    me = lax.axis_index("sp")
    my_chip, core = me // 2, me % 2
    partner = my_chip * 2 + (1 - core)
    n_heads = tot_ref.shape[1]
    n_half = n_heads // 2
    barrier = pltpu.get_barrier_semaphore()
    peers = [partner] + [((my_chip + o) % n_chips) * 2 + core for o in range(1, n_chips)]
    for peer in peers:
        pl.semaphore_signal(barrier, inc=1, device_id={"sp": peer}, device_id_type=MESH)
    pl.semaphore_wait(barrier, len(peers))

    first = pltpu.make_async_remote_copy(tot_ref, part, d2d_sem.at[0], d2d_sem.at[1], device_id={"sp": partner}, device_id_type=MESH)
    first.start()
    first.wait()
    mine = pl.ds(core * n_half, n_half)
    chip[...] = tot_ref[:, mine] + part[:, mine]
    copies = []
    for o in range(1, n_chips):
        target = (my_chip + o) % n_chips
        kind = jnp.where(target > my_chip, 0, 1)
        copy = pltpu.make_async_remote_copy(chip.at[kind], recv.at[o - 1], send_sem.at[o - 1], recv_sem.at[o - 1],
                                            device_id={"sp": target * 2 + core}, device_id_type=MESH)
        copy.start()
        copies.append(copy)
    fwd = jnp.zeros_like(recv[0])
    rev = jnp.zeros_like(recv[0])
    for o in range(1, n_chips):
        copies[o - 1].wait()
        source = (my_chip + n_chips - o) % n_chips
        early = (source < my_chip).astype(F32)
        fwd = fwd + early * recv[o - 1]
        rev = rev + (1.0 - early) * recv[o - 1]
    half[0, 0] = fwd
    half[0, 1] = rev
    last = pltpu.make_async_remote_copy(half.at[0], half.at[1], half_sem.at[0], half_sem.at[1], device_id={"sp": partner}, device_id_type=MESH)
    last.start()
    last.wait()
    other = pl.ds((1 - core) * n_half, n_half)
    is_second = core.astype(F32)
    for slot, rows in ((0, mine), (1, other)):
        init_ref[0, rows] = half[slot, 0] + is_second * part[0, rows]
        init_ref[1, rows] = half[slot, 1] + (1.0 - is_second) * part[1, rows] + tot_ref[1, rows]


def attention_kernel(att_scale, q_ref, k_ref, v_ref, do_ref, init_ref, o_ref, dq_ref, dk_ref, dv_ref, state):
    @pl.when(pl.program_id(1) == 0)
    def _():
        state[...] = init_ref[...]

    n_rows, width = q_ref.shape
    row_id = lax.broadcasted_iota(jnp.int32, (BLOCK_LEN, BLOCK_LEN), 0)
    col_id = lax.broadcasted_iota(jnp.int32, (BLOCK_LEN, BLOCK_LEN), 1)
    causal = row_id >= col_id
    for h in range(width // HEAD_DIM):
        cols = slice(h * HEAD_DIM, (h + 1) * HEAD_DIM)
        s_run = state[0, h]
        r_run = state[1, h]
        for b in range(n_rows // BLOCK_LEN):
            rows = slice(b * BLOCK_LEN, (b + 1) * BLOCK_LEN)
            q, k, v, do = q_ref[rows, cols], k_ref[rows, cols], v_ref[rows, cols], do_ref[rows, cols]
            r_run = r_run - dot_tn(q, do)
            s16, r16 = s_run.astype(BF16), r_run.astype(BF16)
            a = jnp.where(causal, dot_nt(q, k), 0.0).astype(BF16)
            g = jnp.where(causal, dot_nt(do, v), 0.0).astype(BF16)
            o_ref[rows, cols] = (att_scale * (dot(a, v) + dot(q, s16))).astype(BF16)
            dq_ref[rows, cols] = (att_scale * (dot(g, k) + dot_nt(do, s16))).astype(BF16)
            dk_ref[rows, cols] = (att_scale * (dot_tn(g, q) + dot_nt(v, r16))).astype(BF16)
            dv_ref[rows, cols] = (att_scale * (dot_tn(a, do) + dot(k, r16))).astype(BF16)
            s_run = s_run + dot_tn(k, v)
        state[0, h] = s_run
        state[1, h] = r_run


def solution(mesh):
    n_seq = mesh.shape["sp"]
    row_spec = P(("dp", "sp"), None)
    grad_spec = P("dp", None)

    def local_layer(tokens, w_q, w_k, w_v, w_o, grad_y):
        n_rows, dim = tokens.shape
        n_heads = dim // HEAD_DIM
        att_scale = 1.0 / math.sqrt(n_rows * n_seq * HEAD_DIM)
        tile = 512
        rows_bf16 = jax.ShapeDtypeStruct((n_rows, dim), BF16)
        row_tile = pl.BlockSpec((tile, dim), lambda i: (i, 0))
        whole_w = pl.BlockSpec((dim, dim), lambda i: (0, 0), pipeline_mode=pl.Buffered(1))
        state_shape = (2, n_heads, HEAD_DIM, HEAD_DIM)
        q, k, v, do, totals = pl.pallas_call(
            project_kernel,
            grid=(n_rows // tile,),
            in_specs=[row_tile, row_tile] + [whole_w] * 4,
            out_specs=[row_tile] * 4 + [pl.BlockSpec(state_shape, lambda i: (0, 0, 0, 0))],
            out_shape=[rows_bf16] * 4 + [jax.ShapeDtypeStruct(state_shape, F32)],
            compiler_params=pltpu.CompilerParams(vmem_limit_bytes=VMEM_LIMIT, dimension_semantics=("arbitrary",)),
            name="project",
        )(tokens, grad_y, w_q, w_k, w_v, w_o)

        n_chips = n_seq // 2
        half_shape = (n_heads // 2, HEAD_DIM, HEAD_DIM)
        vmem = pl.BlockSpec(memory_space=pltpu.VMEM)
        init = pl.pallas_call(
            functools.partial(exchange_kernel, n_chips),
            in_specs=[vmem],
            out_specs=vmem,
            out_shape=jax.ShapeDtypeStruct(state_shape, F32),
            scratch_shapes=[
                pltpu.VMEM(state_shape, F32),
                pltpu.VMEM((2,) + half_shape, F32),
                pltpu.VMEM((n_chips - 1,) + half_shape, F32),
                pltpu.VMEM((2, 2) + half_shape, F32),
                pltpu.SemaphoreType.DMA((2,)),
                pltpu.SemaphoreType.DMA((n_chips - 1,)),
                pltpu.SemaphoreType.DMA((n_chips - 1,)),
                pltpu.SemaphoreType.DMA((2,)),
            ],
            compiler_params=pltpu.CompilerParams(vmem_limit_bytes=32 * 1024 * 1024, collective_id=0, has_side_effects=True),
            name="exchange",
        )(totals)

        width, chunk = 2 * HEAD_DIM, 512
        col_tile = pl.BlockSpec((chunk, width), lambda g, i: (i, g))
        o, dq, dk, dv = pl.pallas_call(
            functools.partial(attention_kernel, att_scale),
            grid=(dim // width, n_rows // chunk),
            in_specs=[col_tile] * 4 + [pl.BlockSpec((2, width // HEAD_DIM, HEAD_DIM, HEAD_DIM), lambda g, i: (0, g, 0, 0))],
            out_specs=[col_tile] * 4,
            out_shape=[rows_bf16] * 4,
            scratch_shapes=[pltpu.VMEM((2, width // HEAD_DIM, HEAD_DIM, HEAD_DIM), F32)],
            compiler_params=pltpu.CompilerParams(vmem_limit_bytes=32 * 1024 * 1024, dimension_semantics=("arbitrary", "arbitrary")),
            name="attention",
        )(q, k, v, do, init)

        def weight_grad(left, right):
            return jnp.einsum("nd,ne->de", left, right, preferred_element_type=F32)

        def back_proj(rows, weight):
            return jnp.einsum("ne,de->nd", rows, weight, preferred_element_type=F32)

        grads = lax.psum((weight_grad(tokens, dq), weight_grad(tokens, dk), weight_grad(tokens, dv), weight_grad(o, grad_y)), "sp")
        out_y = jnp.dot(o, w_o, preferred_element_type=F32).astype(BF16)
        grad_x = (back_proj(dq, w_q) + back_proj(dk, w_k) + back_proj(dv, w_v)).astype(BF16)
        return (out_y, grad_x) + tuple(grads)

    return jax.shard_map(local_layer, mesh=mesh, in_specs=(row_spec, P(), P(), P(), P(), row_spec),
                         out_specs=(row_spec, row_spec) + (grad_spec,) * 4, check_vma=False)
```

time: 840 us -> 412 us (0.49)
  matrix products: 364 us -> 108 us
  Pallas kernels: 0 us -> 143 us
  local copies, waits for them, and re-layouts: 143 us -> 23.6 us
  waiting for transfers between devices: 221 us -> 115 us
  starting transfers between devices: 44.2 us -> 0.06 us
  other arithmetic: 41.6 us -> 0.01 us
    dot_general x24 -> x8, matrix products: 364 us -> 108 us  [the longest x4 46.5 us: weight_grad(): return jnp.einsum('nd,ne->de', left, right, preferred_element_type=F32)]
    pallas_call x0 -> x3, Pallas kernels: none -> 143 us  [the longest x1 73.2 us: local_layer(): pl.pallas_call(functools.partial(attention_kernel, att_scale), grid=(dim...]
    ppermute x14 -> x0, waiting for transfers between devices: 101 us -> none  [the longest x7 58.9 us: rev_hop(): return lax.ppermute(carried + qdo_total, 'sp', perm=rev_perm)]
    convert_element_type x4 -> x0, local copies, waits for them, and re-layouts: 49.5 us -> none  [to_rows(): return (tensor * att_scale).astype(jnp.bfloat16).reshape(n_rows, model_dim)]
    ppermute x14 -> x0, starting transfers between devices: 44.1 us -> none  [the longest x7 28.5 us: fwd_hop(): return lax.ppermute(carried + kv_total, 'sp', perm=fwd_perm)]
    reshape x3 -> x0, local copies, waits for them, and re-layouts: 37.3 us -> none  [split_heads(): return tensor.reshape(n_blocks, BLOCK_LEN, n_heads, HEAD_DIM)]
    unnamed x26 -> x34, local copies, waits for them, and re-layouts: 56.1 us -> 23.6 us
    another operation x2 -> x0, other arithmetic: 29.6 us -> none  [the longest x1 15.1 us: local_layer(): jnp.cumsum(block_kv, axis=0)]
  transfers between devices with their start and end apart: 15 -> 1, of which waited for: 15 -> 1; matrix products, arithmetic and copies ran while one was open for 7% -> 15% of each run, Pallas kernels for 0% -> 0%
where the time goes in v1:
time: 412 us; the launch traced here: 404 us
  Pallas kernels  143 us (35%)
  waiting for transfers between devices  115 us (28%)
  matrix products  108 us (26%)
  local copies, waits for them, and re-layouts  23.6 us (6%)
  between operations  14.3 us (3%)
    psum x1, waiting for transfers between devices, local_layer(): lax.psum((weight_grad(tokens, dq), weight_grad(tokens, dk), weight_grad(t...  115 us
    pallas_call x1, Pallas kernels, local_layer(): pl.pallas_call(functools.partial(attention_kernel, att_scale), grid=(dim...  73.2 us
    pallas_call x1, Pallas kernels, local_layer(): pl.pallas_call(project_kernel, grid=(n_rows // tile,), in_specs=[row_tile...  46.9 us
    dot_general x4, matrix products, weight_grad(): return jnp.einsum('nd,ne->de', left, right, preferred_element_type=F32)  46.5 us
    dot_general x3, matrix products, back_proj(): return jnp.einsum('ne,de->nd', rows, weight, preferred_element_type=F32)  46.2 us
    unnamed x34, local copies, waits for them, and re-layouts  23.6 us
    pallas_call x1, Pallas kernels, local_layer(): pl.pallas_call(functools.partial(exchange_kernel, n_chips), in_specs=[vme...  22.9 us
    dot_general x1, matrix products, local_layer(): out_y = jnp.dot(o, w_o, preferred_element_type=F32).astype(BF16)  15.2 us
  transfers between devices with their start and end apart: 1, of which 1 were waited for; matrix products, arithmetic and copies ran while one was open for 15% of the time, Pallas kernels for 0%

profile of v1, /device:TPU:81, one launch (start us, length us, event | category | flops | bytes accessed | tf_op | source)
XLA Modules:
  0.0 404.1 jit_solution(11740402548041656223)
XLA Ops:
  7.2 0.1 all-reduce.3.cloned.1.call-start
  7.2 46.9 %project.1 = (bf16[4096,1024]{1,0:T(8,128)(2,1)}, bf16[4096,1024]{1,0:T(8,128)(2,1)}, bf16[4096,1024]{1,0:T(8,128)(2,1)}, bf16[4096,1024]{1,0:T(8,128)(2,1)}, f32[2,8,128,128]{3,2,1,0:T(8,128)}) custom-call(bf16[4096,1024]{1,0:T(8,128)(2,1)} %x_ref.1, bf16[4096,1024]{1,0:T(8,128)(2,1)} %dy_ref.1, bf16[1024,1024]{1,0:T(8,128)(2,1)} %wq_ref.1, ...), custom_call_target="tpu_custom_call" | custom-call | tf_op jit(solution)/shard_map/project/pallas_call | solution.py:135
  54.2 0.0 copy-start
  54.2 1.2 copy-done
  55.4 0.0 slice-start.2
  55.4 22.9 %exchange.1.init_ref = f32[2,8,128,128]{3,2,1,0:T(8,128)S(1)} custom-call(f32[2,8,128,128]{3,2,1,0:T(8,128)S(1)} %copy-done), custom_call_target="tpu_custom_call" | custom-call | tf_op jit(solution)/shard_map/exchange/pallas_call | solution.py:148
  78.3 0.0 slice-start.3
  78.3 73.2 %attention.1 = (bf16[4096,1024]{1,0:T(8,128)(2,1)S(1)}, bf16[4096,1024]{1,0:T(8,128)(2,1)S(1)}, bf16[4096,1024]{1,0:T(8,128)(2,1)}, bf16[4096,1024]{1,0:T(8,128)(2,1)}) custom-call(bf16[4096,1024]{1,0:T(8,128)(2,1)} %get-tuple-element.15.q_ref, bf16[4096,1024]{1,0:T(8,128)(2,1)} %get-tuple-element.16.k_ref, bf16[4096,1024]{1,0:T(8,128)(2,1)} %get-tuple-element.17.v_ref, ...), custom_call_target="tpu_custom_call" | custom-call | tf_op jit(solution)/shard_map/attention/pallas_call | solution.py:169
  151.5 0.0 copy-start.2
  151.5 0.0 copy-start.1
  151.5 0.0 slice-done.2
  151.6 0.0 slice-done.3
  151.6 0.0 slice-start.4
  151.6 10.5 %fusion.2 = f32[1024,1024]{1,0:T(8,128)} fusion(bf16[4096,1024]{1,0:T(8,128)(2,1)S(1)} %get-tuple-element.20, bf16[4096,1024]{1,0:T(8,128)(2,1)S(1)} %bitcast.25), kind=kOutput, calls=%fused_computation.7 | convolution fusion | flops 8589934592 | bytes 20971520 | tf_op jit(solution)/shard_map/nd,ne->de/dot_general | solution.py:181
  162.0 0.0 copy-done.2
  162.0 0.0 copy-done.1
  162.0 0.0 slice-start.5
  162.0 0.0 slice-start.6
  162.1 13.0 %convolution_bitcast_fusion.2 = f32[1024,1024]{0,1:T(8,128)} fusion(bf16[4096,1024]{1,0:T(8,128)(2,1)S(1)} %get-tuple-element.21, bf16[4096,1024]{1,0:T(8,128)(2,1)} %x_ref.1), kind=kOutput, calls=%fused_computation.4 | convolution fusion | flops 8589934592 | bytes 20971520 | tf_op jit(solution)/shard_map/nd,ne->de/dot_general | solution.py:181
  175.0 0.0 slice-done.4
  175.0 0.0 slice-done.5
  175.0 0.0 slice-start.7
  175.0 12.7 %convolution_bitcast_fusion.1 = f32[1024,1024]{0,1:T(8,128)} fusion(bf16[4096,1024]{1,0:T(8,128)(2,1)} %get-tuple-element.22, bf16[4096,1024]{1,0:T(8,128)(2,1)S(1)} %bitcast.27), kind=kOutput, calls=%fused_computation.3 | convolution fusion | flops 8589934592 | bytes 20971520 | tf_op jit(solution)/shard_map/nd,ne->de/dot_general | solution.py:181
  187.7 0.0 slice-done.6
  187.7 0.0 slice-done.7
  187.7 10.4 %convolution_bitcast_fusion = f32[1024,1024]{0,1:T(8,128)} fusion(bf16[4096,1024]{1,0:T(8,128)(2,1)S(1)} %bitcast.29, bf16[4096,1024]{1,0:T(8,128)(2,1)S(1)} %bitcast.27), kind=kOutput, calls=%fused_computation.2 | convolution fusion | flops 8589934592 | bytes 20971520 | tf_op jit(solution)/shard_map/nd,ne->de/dot_general | solution.py:181
  198.2 0.0 copy-start.3
  198.2 0.1 all-reduce.3.cloned.1.call-update
  198.2 1.5 copy-done.3
  199.8 0.0 copy-start.4
  199.8 0.0 slice-start
  199.8 15.2 %convolution_convert_fusion = bf16[4096,1024]{1,0:T(8,128)(2,1)} fusion(bf16[4096,1024]{1,0:T(8,128)(2,1)} %copy-done.2, bf16[1024,1024]{1,0:T(8,128)(2,1)S(1)} %copy-done.3), kind=kOutput, calls=%fused_computation.1 | convolution fusion | flops 8594128896 | bytes 18874368 | tf_op jit(solution)/shard_map/dot_general | solution.py:187
  214.9 0.0 copy-done.4
  214.9 0.0 slice-start.1
  214.9 0.0 copy-start.5
  214.9 14.7 %fusion.1 = f32[4096,1024]{1,0:T(8,128)} fusion(bf16[4096,1024]{1,0:T(8,128)(2,1)} %get-tuple-element.22, bf16[1024,1024]{1,0:T(8,128)(2,1)S(1)} %copy-done.4), kind=kOutput, calls=%fused_computation.6 | convolution fusion | flops 8589934592 | bytes 27262976 | tf_op jit(solution)/shard_map/ne,de->nd/dot_general | solution.py:184
  229.6 0.0 slice-done
  229.6 0.0 slice-done.1
  229.6 0.0 copy-done.5
  229.7 0.0 copy-start.6
  229.7 11.8 %fusion = f32[4096,1024]{1,0:T(8,128)} fusion(bf16[4096,1024]{1,0:T(8,128)(2,1)S(1)} %bitcast.23, bf16[1024,1024]{1,0:T(8,128)(2,1)S(1)} %copy-done.5), kind=kOutput, calls=%fused_computation.5 | convolution fusion | flops 8589934592 | bytes 27262976 | tf_op jit(solution)/shard_map/ne,de->nd/dot_general | solution.py:184
  241.5 0.0 copy-done.6
  241.5 19.7 %add_convert_fusion = bf16[4096,1024]{1,0:T(8,128)(2,1)} fusion(f32[4096,1024]{1,0:T(8,128)} %fusion, f32[4096,1024]{1,0:T(8,128)} %fusion.1, bf16[4096,1024]{1,0:T(8,128)(2,1)} %get-tuple-element.23, bf16[1024,1024]{1,0:T(8,128)(2,1)S(1)} %copy-done.6), kind=kOutput, calls=%fused_computation | convolution fusion | flops 8602517504 | bytes 52428800 | tf_op jit(solution)/shard_map/ne,de->nd/dot_general | solution.py:184
  261.2 115.1 %all-reduce.3.cloned.1.call-done = (f32[1024,1024]{0,1:T(8,128)}, f32[1024,1024]{0,1:T(8,128)}, f32[1024,1024]{0,1:T(8,128)}, f32[1024,1024]{1,0:T(8,128)}) async-done(((f32[1024,1024]{0,1:T(8,128)}, f32[1024,1024]{0,1:T(8,128)}, f32[1024,1024]{0,1:T(8,128)}, f32[1024,1024]{1,0:T(8,128)}), (f32[1024,1024]{0,1:T(8,128)}, f32[1024,1024]{0,1:T(8,128)}, f32[1024,1024]{0,1:T(8,128)}, ...) | async-done | bytes 16777232 | tf_op jit(solution)/shard_map/psum | solution.py:186
  376.3 5.3 %copy.12 = f32[1024,1024]{1,0:T(8,128)} copy(f32[1024,1024]{0,1:T(8,128)} %get-tuple-element.30) | data formatting | bytes 8388608
  381.6 5.3 %copy.13 = f32[1024,1024]{1,0:T(8,128)} copy(f32[1024,1024]{0,1:T(8,128)} %get-tuple-element.31) | data formatting | bytes 8388608
  387.0 5.3 %copy.14 = f32[1024,1024]{1,0:T(8,128)} copy(f32[1024,1024]{0,1:T(8,128)} %get-tuple-element.32) | data formatting | bytes 8388608
  392.3 4.8 %copy.19 = f32[1024,1024]{1,0:T(8,128)} copy(f32[1024,1024]{1,0:T(8,128)} %get-tuple-element.39) | data formatting | bytes 8388608
  (4 shorter events, 0.0 us)
Async XLA Ops:
  7.2 369.1 %all-reduce.3.cloned.1.call-start = ((), (), s32[]{:S(2)}) async-start(), calls=%async_computation | async-start | bytes 33554432 | tf_op jit(solution)/shard_map/psum | solution.py:186
  54.2 1.2 copy-start
  55.4 96.1 %slice-start.2 = ((s8[8388608]{0:T(1024)(128)(4,1)}), s8[4194304]{0:T(1024)(128)(4,1)S(1)}, s32[]{:S(2)}) async-start(s8[8388608]{0:T(1024)(128)(4,1)} %bitcast.24), calls=%async_computation.3 | async-start | bytes 8388608
  78.3 73.2 %slice-start.3 = ((s8[8388608]{0:T(1024)(128)(4,1)}), s8[4194304]{0:T(1024)(128)(4,1)S(1)}, s32[]{:S(2)}) async-start(s8[8388608]{0:T(1024)(128)(4,1)} %bitcast.24), calls=%async_computation.4 | async-start | bytes 8388608
  151.5 10.5 %copy-start.2 = (bf16[4096,1024]{1,0:T(8,128)(2,1)}, bf16[4096,1024]{1,0:T(8,128)(2,1)S(1)}, u32[]{:S(2)}) copy-start(bf16[4096,1024]{1,0:T(8,128)(2,1)S(1)} %get-tuple-element.20) | copy-start | bytes 25165828
  151.5 10.5 %copy-start.1 = (bf16[4096,1024]{1,0:T(8,128)(2,1)}, bf16[4096,1024]{1,0:T(8,128)(2,1)S(1)}, u32[]{:S(2)}) copy-start(bf16[4096,1024]{1,0:T(8,128)(2,1)S(1)} %get-tuple-element.21) | copy-start | bytes 25165828
  151.6 23.4 %slice-start.4 = ((s8[8388608]{0:T(1024)(128)(4,1)}), s8[4194304]{0:T(1024)(128)(4,1)S(1)}, s32[]{:S(2)}) async-start(s8[8388608]{0:T(1024)(128)(4,1)} %bitcast.26), calls=%async_computation.5 | async-start | bytes 8388608
  162.0 13.0 %slice-start.5 = ((s8[8388608]{0:T(1024)(128)(4,1)}), s8[4194304]{0:T(1024)(128)(4,1)S(1)}, s32[]{:S(2)}) async-start(s8[8388608]{0:T(1024)(128)(4,1)} %bitcast.26), calls=%async_computation.6 | async-start | bytes 8388608
  162.0 25.7 %slice-start.6 = ((s8[8388608]{0:T(1024)(128)(4,1)}), s8[4194304]{0:T(1024)(128)(4,1)S(1)}, s32[]{:S(2)}) async-start(s8[8388608]{0:T(1024)(128)(4,1)} %bitcast.28), calls=%async_computation.7 | async-start | bytes 8388608
  175.0 12.7 %slice-start.7 = ((s8[8388608]{0:T(1024)(128)(4,1)}), s8[4194304]{0:T(1024)(128)(4,1)S(1)}, s32[]{:S(2)}) async-start(s8[8388608]{0:T(1024)(128)(4,1)} %bitcast.28), calls=%async_computation.8 | async-start | bytes 8388608
  198.2 1.6 copy-start.3
  199.8 15.2 %copy-start.4 = (bf16[1024,1024]{1,0:T(8,128)(2,1)S(1)}, bf16[1024,1024]{1,0:T(8,128)(2,1)}, u32[]{:S(2)}) copy-start(bf16[1024,1024]{1,0:T(8,128)(2,1)} %wk_ref.1) | copy-start | bytes 6291460
  199.8 29.9 %slice-start = ((s8[8388608]{0:T(1024)(128)(4,1)}), s8[4194304]{0:T(1024)(128)(4,1)S(1)}, s32[]{:S(2)}) async-start(s8[8388608]{0:T(1024)(128)(4,1)} %bitcast.22), calls=%async_computation.1 | async-start | bytes 8388608
  214.9 14.7 %slice-start.1 = ((s8[8388608]{0:T(1024)(128)(4,1)}), s8[4194304]{0:T(1024)(128)(4,1)S(1)}, s32[]{:S(2)}) async-start(s8[8388608]{0:T(1024)(128)(4,1)} %bitcast.22), calls=%async_computation.2 | async-start | bytes 8388608
  214.9 14.7 %copy-start.5 = (bf16[1024,1024]{1,0:T(8,128)(2,1)S(1)}, bf16[1024,1024]{1,0:T(8,128)(2,1)}, u32[]{:S(2)}) copy-start(bf16[1024,1024]{1,0:T(8,128)(2,1)} %wq_ref.1) | copy-start | bytes 6291460
  229.7 11.8 %copy-start.6 = (bf16[1024,1024]{1,0:T(8,128)(2,1)S(1)}, bf16[1024,1024]{1,0:T(8,128)(2,1)}, u32[]{:S(2)}) copy-start(bf16[1024,1024]{1,0:T(8,128)(2,1)} %wv_ref.1) | copy-start | bytes 6291460
Sparse Core Ops, SparseCore 0:
  198.3 177.8 all-reduce.2

commit v2 on v1

--- a/solution.py
+++ b/solution.py
@@ -12,6 +12,9 @@
 BF16 = jnp.bfloat16
 F32 = jnp.float32
 MESH = pl.DeviceIdType.MESH
+CHUNKS = 8
+TILE = 256
+AT = (0, 1, 4, 8, 12, 15, 16)
 VMEM_LIMIT = 64 * 1024 * 1024 - 1024 * 64
 
 
@@ -89,33 +92,224 @@
         init_ref[1, rows] = half[slot, 1] + (1.0 - is_second) * part[1, rows] + tot_ref[1, rows]
 
 
-def attention_kernel(att_scale, q_ref, k_ref, v_ref, do_ref, init_ref, o_ref, dq_ref, dk_ref, dv_ref, state):
-    @pl.when(pl.program_id(1) == 0)
-    def _():
-        state[...] = init_ref[...]
-
-    n_rows, width = q_ref.shape
-    row_id = lax.broadcasted_iota(jnp.int32, (BLOCK_LEN, BLOCK_LEN), 0)
-    col_id = lax.broadcasted_iota(jnp.int32, (BLOCK_LEN, BLOCK_LEN), 1)
-    causal = row_id >= col_id
-    for h in range(width // HEAD_DIM):
-        cols = slice(h * HEAD_DIM, (h + 1) * HEAD_DIM)
-        s_run = state[0, h]
-        r_run = state[1, h]
-        for b in range(n_rows // BLOCK_LEN):
-            rows = slice(b * BLOCK_LEN, (b + 1) * BLOCK_LEN)
-            q, k, v, do = q_ref[rows, cols], k_ref[rows, cols], v_ref[rows, cols], do_ref[rows, cols]
-            r_run = r_run - dot_tn(q, do)
-            s16, r16 = s_run.astype(BF16), r_run.astype(BF16)
-            a = jnp.where(causal, dot_nt(q, k), 0.0).astype(BF16)
-            g = jnp.where(causal, dot_nt(do, v), 0.0).astype(BF16)
-            o_ref[rows, cols] = (att_scale * (dot(a, v) + dot(q, s16))).astype(BF16)
-            dq_ref[rows, cols] = (att_scale * (dot(g, k) + dot_nt(do, s16))).astype(BF16)
-            dk_ref[rows, cols] = (att_scale * (dot_tn(g, q) + dot_nt(v, r16))).astype(BF16)
-            dv_ref[rows, cols] = (att_scale * (dot_tn(a, do) + dot(k, r16))).astype(BF16)
-            s_run = s_run + dot_tn(k, v)
-        state[0, h] = s_run
-        state[1, h] = r_run
+def layer_kernel(att_scale, n_chips, n_groups, q_ref, k_ref, v_ref, do_ref, x_ref, dy_ref, init_ref, wq_hbm, wk_hbm, wv_hbm, wo_hbm,
+                 y_ref, dx_ref, grad_hbm, rows_hbm,
+                 state, stage, part, pair, near, own, weights, tiles,
+                 stage_sem, weight_sem, tile_sem, local_sem, send_sem, recv_sem):
+    step = pl.program_id(0)
+    me = lax.axis_index("sp")
+    chip, core = me // 2, me % 2
+    partner = chip * 2 + (1 - core)
+    right_chip, left_chip, far_chip = (chip + 1) % n_chips, (chip + n_chips - 1) % n_chips, (chip + 2) % n_chips
+    right, left = right_chip * 2 + core, left_chip * 2 + core
+    n_chunks = CHUNKS
+    att_steps = n_groups * n_chunks
+    chunk, width = q_ref.shape
+    core_rows = part.shape[1] // 2
+    chip_rows = core_rows // n_chips
+    half_rows = chip_rows // 2
+
+    def rows_of(owner, half=None, of_core=None):
+        base = (core if of_core is None else of_core) * core_rows + owner * chip_rows
+        if half is None:
+            return pl.ds(pl.multiple_of(base, half_rows), chip_rows)
+        return pl.ds(pl.multiple_of(base + half * half_rows, half_rows), half_rows)
+
+    def remote(kind, g, src, dst, target):
+        return pltpu.make_async_remote_copy(src, dst, send_sem.at[kind, g], recv_sem.at[kind, g],
+                                            device_id={"sp": target}, device_id_type=MESH)
+
+    def message(kind, g):
+        if kind == 0:
+            other = pl.ds(pl.multiple_of((1 - core) * core_rows, core_rows), core_rows)
+            return remote(0, g, part.at[g, other], pair.at[g % 2], partner)
+        if kind in (1, 2):
+            to, half = ((right, 0), (left, 1))[kind - 1]
+            return remote(kind, g, part.at[g, rows_of(far_chip, half)], near.at[g, half], to)
+        if kind in (3, 4):
+            to, owner = ((right, right_chip), (left, left_chip))[kind - 3]
+            return remote(kind, g, part.at[g, rows_of(owner)], own.at[g, kind - 3], to)
+        if kind in (5, 6, 7):
+            to = (right, left, partner)[kind - 5]
+            return remote(kind, g, part.at[g, rows_of(chip)], grad_hbm.at[g, rows_of(chip)], to)
+        if kind in (8, 9):
+            to, rows = ((right, rows_of(left_chip, 0)), (left, rows_of(right_chip, 1)))[kind - 8]
+        else:
+            to, rows = partner, rows_of((left_chip, right_chip, far_chip)[kind - 10])
+        return remote(kind, g, grad_hbm.at[g, rows], grad_hbm.at[g, rows], to)
+
+    def local(g):
+        return pltpu.make_async_copy(part.at[g, rows_of(chip)], grad_hbm.at[g, rows_of(chip)], local_sem.at[g])
+
+    def event(offset):
+        late = step - offset
+        return (late >= 0) & (late < att_steps) & (late % n_chunks == 0), late // n_chunks
+
+    @pl.when(step == 0)
+    def _():
+        barrier = pltpu.get_barrier_semaphore()
+        for peer in (partner, right, left):
+            pl.semaphore_signal(barrier, inc=1, device_id={"sp": peer}, device_id_type=MESH)
+        pl.semaphore_wait(barrier, 3)
+        for i, w in enumerate((wq_hbm, wk_hbm, wv_hbm, wo_hbm)):
+            pltpu.make_async_copy(w, weights.at[i], weight_sem.at[i]).start()
+
+    due, g0 = event(n_chunks + AT[0])
+
+    @pl.when(due)
+    def _():
+        message(0, g0).start()
+
+    due, g1 = event(n_chunks + AT[1])
+
+    @pl.when(due)
+    def _():
+        message(0, g1).wait_recv()
+        mine = pl.ds(pl.multiple_of(core * core_rows, core_rows), core_rows)
+        part[g1, mine] += pair[g1 % 2]
+        message(1, g1).start()
+        message(2, g1).start()
+
+    due, g2 = event(n_chunks + AT[2])
+
+    @pl.when(due)
+    def _():
+        message(1, g2).wait_recv()
+        message(2, g2).wait_recv()
+        part[g2, rows_of(right_chip, 0)] += near[g2, 0]
+        part[g2, rows_of(left_chip, 1)] += near[g2, 1]
+        message(3, g2).start()
+        message(4, g2).start()
+
+    due, g3 = event(n_chunks + AT[3])
+
+    @pl.when(due)
+    def _():
+        message(3, g3).wait_recv()
+        message(4, g3).wait_recv()
+        part[g3, rows_of(chip)] += own[g3, 0] + own[g3, 1]
+        for kind in (5, 6, 7):
+            message(kind, g3).start()
+        local(g3).start()
+
+    due, g4 = event(n_chunks + AT[4])
+
+    @pl.when(due)
+    def _():
+        message(5, g4).wait_recv()
+        message(6, g4).wait_recv()
+        for kind in (8, 9, 10, 11):
+            message(kind, g4).start()
+
+    due, g5 = event(n_chunks + AT[5])
+
+    @pl.when(due)
+    def _():
+        message(8, g5).wait_recv()
+        message(9, g5).wait_recv()
+        message(12, g5).start()
+
+    due, g6 = event(n_chunks + AT[6])
+
+    @pl.when(due)
+    def _():
+        for kind in (7, 10, 11, 12):
+            message(kind, g6).wait_recv()
+        local(g6).wait()
+        for kind in range(13):
+            message(kind, g6).wait_send()
+
+    def put_stage(s):
+        rows = pl.ds(pl.multiple_of((s % n_chunks) * chunk, chunk), chunk)
+        return pltpu.make_async_copy(stage.at[s % 2], rows_hbm.at[s // n_chunks, rows], stage_sem.at[s % 2])
+
+    tile_rows = tiles.shape[2]
+    n_tiles = n_chunks * chunk // tile_rows
+
+    def get_tile(t):
+        rows = pl.ds(pl.multiple_of(t * tile_rows, tile_rows), tile_rows)
+        return pltpu.make_async_copy(rows_hbm.at[:, rows], tiles.at[t % 2], tile_sem.at[t % 2])
+
+    @pl.when((step >= 2) & (step < att_steps + 2))
+    def _():
+        put_stage(step - 2).wait()
+
+    @pl.when(step < att_steps)
+    def _():
+        @pl.when(step % n_chunks == 0)
+        def _():
+            state[...] = init_ref[...]
+
+        slot = step % 2
+        row_id = lax.broadcasted_iota(jnp.int32, (BLOCK_LEN, BLOCK_LEN), 0)
+        col_id = lax.broadcasted_iota(jnp.int32, (BLOCK_LEN, BLOCK_LEN), 1)
+        causal = row_id >= col_id
+        for h in range(width // HEAD_DIM):
+            cols = slice(h * HEAD_DIM, (h + 1) * HEAD_DIM)
+            s_run = state[0, h]
+            r_run = state[1, h]
+            for b in range(chunk // BLOCK_LEN):
+                rows = slice(b * BLOCK_LEN, (b + 1) * BLOCK_LEN)
+                q, k, v, do = q_ref[rows, cols], k_ref[rows, cols], v_ref[rows, cols], do_ref[rows, cols]
+                r_run = r_run - dot_tn(q, do)
+                s16, r16 = s_run.astype(BF16), r_run.astype(BF16)
+                a = jnp.where(causal, dot_nt(q, k), 0.0).astype(BF16)
+                e = jnp.where(causal, dot_nt(do, v), 0.0).astype(BF16)
+
+                def put(i, value):
+                    stage[slot, rows, i * width + h * HEAD_DIM:i * width + (h + 1) * HEAD_DIM] = (att_scale * value).astype(BF16)
+
+                put(0, dot(e, k) + dot_nt(do, s16))
+                put(1, dot_tn(e, q) + dot_nt(v, r16))
+                put(2, dot_tn(a, do) + dot(k, r16))
+                put(3, dot(a, v) + dot(q, s16))
+                s_run = s_run + dot_tn(k, v)
+            state[0, h] = s_run
+            state[1, h] = r_run
+        put_stage(step).start()
+        g = step // n_chunks
+        qkv = 3 * width
+
+        @pl.when(step % n_chunks == 0)
+        def _():
+            part[g, :, :qkv] = dot_tn(x_ref[...], stage[slot, :, :qkv])
+            part[g, :, qkv:] = dot_tn(dy_ref[...], stage[slot, :, qkv:])
+
+        @pl.when(step % n_chunks > 0)
+        def _():
+            part[g, :, :qkv] += dot_tn(x_ref[...], stage[slot, :, :qkv])
+            part[g, :, qkv:] += dot_tn(dy_ref[...], stage[slot, :, qkv:])
+
+    tile = step - att_steps - 2
+
+    @pl.when(tile == -1)
+    def _():
+        get_tile(0).start()
+        for i, w in enumerate((wq_hbm, wk_hbm, wv_hbm, wo_hbm)):
+            pltpu.make_async_copy(w, weights.at[i], weight_sem.at[i]).wait()
+
+    @pl.when((tile >= 0) & (tile < n_tiles))
+    def _():
+        @pl.when(tile + 1 < n_tiles)
+        def _():
+            get_tile(tile + 1).start()
+
+        get_tile(tile).wait()
+
+        def gather(i):
+            return jnp.concatenate([tiles[tile % 2, g, :, i * width:(i + 1) * width] for g in range(n_groups)], axis=1)
+
+        dx_ref[...] = (dot_nt(gather(0), weights[0]) + dot_nt(gather(1), weights[1]) + dot_nt(gather(2), weights[2])).astype(BF16)
+        y_ref[...] = dot(gather(3), weights[3]).astype(BF16)
+
+
+def assemble_kernel(n_groups, grad_ref, wq_ref, wk_ref, wv_ref, wo_ref):
+    width = grad_ref.shape[2] // 4
+    for g in range(n_groups):
+        cols = slice(g * width, (g + 1) * width)
+        for i, out in enumerate((wq_ref, wk_ref, wv_ref)):
+            out[:, cols] = grad_ref[g, :, i * width:(i + 1) * width]
+        wo_ref[cols, :] = grad_ref[g, :, 3 * width:].T
 
 
 def solution(mesh):
@@ -164,28 +358,61 @@
             name="exchange",
         )(totals)
 
-        width, chunk = 2 * HEAD_DIM, 512
-        col_tile = pl.BlockSpec((chunk, width), lambda g, i: (i, g))
-        o, dq, dk, dv = pl.pallas_call(
-            functools.partial(attention_kernel, att_scale),
-            grid=(dim // width, n_rows // chunk),
-            in_specs=[col_tile] * 4 + [pl.BlockSpec((2, width // HEAD_DIM, HEAD_DIM, HEAD_DIM), lambda g, i: (0, g, 0, 0))],
-            out_specs=[col_tile] * 4,
-            out_shape=[rows_bf16] * 4,
-            scratch_shapes=[pltpu.VMEM((2, width // HEAD_DIM, HEAD_DIM, HEAD_DIM), F32)],
-            compiler_params=pltpu.CompilerParams(vmem_limit_bytes=32 * 1024 * 1024, dimension_semantics=("arbitrary", "arbitrary")),
-            name="attention",
-        )(q, k, v, do, init)
-
-        def weight_grad(left, right):
-            return jnp.einsum("nd,ne->de", left, right, preferred_element_type=F32)
-
-        def back_proj(rows, weight):
-            return jnp.einsum("ne,de->nd", rows, weight, preferred_element_type=F32)
-
-        grads = lax.psum((weight_grad(tokens, dq), weight_grad(tokens, dk), weight_grad(tokens, dv), weight_grad(o, grad_y)), "sp")
-        out_y = jnp.dot(o, w_o, preferred_element_type=F32).astype(BF16)
-        grad_x = (back_proj(dq, w_q) + back_proj(dk, w_k) + back_proj(dv, w_v)).astype(BF16)
+        width, chunk, tile_rows = 2 * HEAD_DIM, n_rows // CHUNKS, TILE
+        n_groups, n_tiles = dim // width, n_rows // TILE
+        att_steps = n_groups * CHUNKS
+        n_steps = max(att_steps + 2 + n_tiles, att_steps + AT[6] + 1)
+
+        def att(s):
+            return jnp.minimum(s, att_steps - 1)
+
+        def tile_index(s):
+            return (jnp.clip(s - att_steps - 2, 0, n_tiles - 1), 0)
+
+        col_tile = pl.BlockSpec((chunk, width), lambda s: (att(s) % CHUNKS, att(s) // CHUNKS))
+        row_chunk = pl.BlockSpec((chunk, dim), lambda s: (att(s) % CHUNKS, 0))
+        init_tile = pl.BlockSpec((2, width // HEAD_DIM, HEAD_DIM, HEAD_DIM), lambda s: (0, att(s) // CHUNKS, 0, 0))
+        hbm = pl.BlockSpec(memory_space=pl.ANY)
+        out_tile = pl.BlockSpec((tile_rows, dim), tile_index)
+        chip_rows = dim // 2 // n_chips
+        n_kinds = 13
+        out_y, grad_x, grads, _ = pl.pallas_call(
+            functools.partial(layer_kernel, att_scale, n_chips, n_groups),
+            grid=(n_steps,),
+            in_specs=[col_tile] * 4 + [row_chunk] * 2 + [init_tile] + [hbm] * 4,
+            out_specs=[out_tile] * 2 + [hbm] * 2,
+            out_shape=[rows_bf16] * 2 + [jax.ShapeDtypeStruct((n_groups, dim, 4 * width), F32),
+                                         jax.ShapeDtypeStruct((n_groups, n_rows, 4 * width), BF16)],
+            scratch_shapes=[
+                pltpu.VMEM((2, width // HEAD_DIM, HEAD_DIM, HEAD_DIM), F32),
+                pltpu.VMEM((2, chunk, 4 * width), BF16),
+                pltpu.VMEM((n_groups, dim, 4 * width), F32),
+                pltpu.VMEM((2, dim // 2, 4 * width), F32),
+                pltpu.VMEM((n_groups, 2, chip_rows // 2, 4 * width), F32),
+                pltpu.VMEM((n_groups, 2, chip_rows, 4 * width), F32),
+                pltpu.VMEM((4, dim, dim), BF16),
+                pltpu.VMEM((2, n_groups, tile_rows, 4 * width), BF16),
+                pltpu.SemaphoreType.DMA((2,)),
+                pltpu.SemaphoreType.DMA((4,)),
+                pltpu.SemaphoreType.DMA((2,)),
+                pltpu.SemaphoreType.DMA((n_groups,)),
+                pltpu.SemaphoreType.DMA((n_kinds, n_groups)),
+                pltpu.SemaphoreType.DMA((n_kinds, n_groups)),
+            ],
+            compiler_params=pltpu.CompilerParams(vmem_limit_bytes=VMEM_LIMIT, dimension_semantics=("arbitrary",), collective_id=1, has_side_effects=True),
+            name="layer",
+        )(q, k, v, do, tokens, grad_y, init, w_q, w_k, w_v, w_o)
+
+        slab = 128
+        grads = pl.pallas_call(
+            functools.partial(assemble_kernel, n_groups),
+            grid=(dim // slab,),
+            in_specs=[pl.BlockSpec((n_groups, slab, 4 * width), lambda i: (0, i, 0))],
+            out_specs=[pl.BlockSpec((slab, dim), lambda i: (i, 0))] * 3 + [pl.BlockSpec((dim, slab), lambda i: (0, i))],
+            out_shape=[jax.ShapeDtypeStruct((dim, dim), F32)] * 4,
+            compiler_params=pltpu.CompilerParams(vmem_limit_bytes=32 * 1024 * 1024, dimension_semantics=("arbitrary",)),
+            name="assemble",
+        )(grads)
         return (out_y, grad_x) + tuple(grads)
 
     return jax.shard_map(local_layer, mesh=mesh, in_specs=(row_spec, P(), P(), P(), P(), row_spec),

time: 412 us -> 316 us (0.77); the launches traced: 404 us -> 316 us
  Pallas kernels: 143 us -> 292 us
  waiting for transfers between devices: 115 us -> 0 us
  matrix products: 108 us -> 0 us
  between operations: 14.3 us -> 0.68 us
    pallas_call x1 -> x2, Pallas kernels: 73.2 us -> 222 us  [the longest x1 215 us: local_layer(): pl.pallas_call(functools.partial(layer_kernel, att_scale, n_chips, n_grou...]
    psum x1 -> x0, waiting for transfers between devices: 115 us -> none  [local_layer(): lax.psum((weight_grad(tokens, dq), weight_grad(tokens, dk), weight_grad(t...]
    dot_general x8 -> x0, matrix products: 108 us -> none  [the longest x4 46.5 us: weight_grad(): return jnp.einsum('nd,ne->de', left, right, preferred_element_type=F32)]
    unnamed x34 -> x8, local copies, waits for them, and re-layouts: 23.6 us -> 23.5 us
  transfers between devices with their start and end apart: 1 -> 0, of which waited for: 1 -> 0; matrix products, arithmetic and copies ran while one was open for 15% -> 0% of each run, Pallas kernels for 0% -> 0%
where the time goes in v2:
time: 316 us
  Pallas kernels  292 us (92%)
  local copies, waits for them, and re-layouts  23.5 us (7%)
    pallas_call x1, Pallas kernels, local_layer(): pl.pallas_call(functools.partial(layer_kernel, att_scale, n_chips, n_grou...  215 us
    pallas_call x1, Pallas kernels, local_layer(): pl.pallas_call(project_kernel, grid=(n_rows // tile,), in_specs=[row_tile...  47 us
    unnamed x8, local copies, waits for them, and re-layouts  23.5 us
    pallas_call x1, Pallas kernels, local_layer(): pl.pallas_call(functools.partial(exchange_kernel, n_chips), in_specs=[vme...  22.8 us
    pallas_call x1, Pallas kernels, local_layer(): pl.pallas_call(functools.partial(assemble_kernel, n_groups), grid=(dim //...  7.05 us

profile of v2, /device:TPU:81, one launch (start us, length us, event | category | flops | bytes accessed | tf_op | source)
XLA Modules:
  0.0 315.7 jit_solution(14094926407549869238)
XLA Ops:
  0.6 47.0 %project.1 = (bf16[4096,1024]{1,0:T(8,128)(2,1)}, bf16[4096,1024]{1,0:T(8,128)(2,1)}, bf16[4096,1024]{1,0:T(8,128)(2,1)}, bf16[4096,1024]{1,0:T(8,128)(2,1)}, f32[2,8,128,128]{3,2,1,0:T(8,128)}) custom-call(bf16[4096,1024]{1,0:T(8,128)(2,1)} %x_ref.3, bf16[4096,1024]{1,0:T(8,128)(2,1)} %dy_ref.3, bf16[1024,1024]{1,0:T(8,128)(2,1)} %wq_hbm.1, ...), custom_call_target="tpu_custom_call" | custom-call | tf_op jit(solution)/shard_map/project/pallas_call | solution.py:329
  47.6 0.0 copy-start.2
  47.6 1.2 copy-done.2
  48.8 22.8 %exchange.1.init_ref = f32[2,8,128,128]{3,2,1,0:T(8,128)S(1)} custom-call(f32[2,8,128,128]{3,2,1,0:T(8,128)S(1)} %copy-done.2), custom_call_target="tpu_custom_call" | custom-call | tf_op jit(solution)/shard_map/exchange/pallas_call | solution.py:342
  71.6 0.0 copy-start.1
  71.7 1.0 copy-done.1
  72.6 214.7 %layer.1 = (bf16[4096,1024]{1,0:T(8,128)(2,1)}, bf16[4096,1024]{1,0:T(8,128)(2,1)}, f32[4,1024,1024]{2,1,0:T(8,128)}, bf16[4,4096,1024]{2,1,0:T(8,128)(2,1)}) custom-call(bf16[4096,1024]{1,0:T(8,128)(2,1)} %get-tuple-element.18.q_ref, bf16[4096,1024]{1,0:T(8,128)(2,1)} %get-tuple-element.19.k_ref, bf16[4096,1024]{1,0:T(8,128)(2,1)} %get-tuple-element.20.v_ref, ...), custom_call_target="tpu_custom_call" | custom-call | tf_op jit(solution)/shard_map/layer/pallas_call | solution.py:379
  287.3 0.0 copy-start
  287.3 5.8 %copy-done = f32[4,1024,1024]{2,1,0:T(8,128)S(1)} copy-done((f32[4,1024,1024]{2,1,0:T(8,128)S(1)}, f32[4,1024,1024]{2,1,0:T(8,128)}, u32[]{:S(2)}) %copy-start) | copy-done | bytes 16777240
  293.1 7.0 %assemble.1 = (f32[1024,1024]{1,0:T(8,128)}, f32[1024,1024]{1,0:T(8,128)}, f32[1024,1024]{1,0:T(8,128)}, f32[1024,1024]{1,0:T(8,128)}) custom-call(f32[4,1024,1024]{2,1,0:T(8,128)S(1)} %copy-done), custom_call_target="tpu_custom_call" | custom-call | tf_op jit(solution)/shard_map/assemble/pallas_call | solution.py:407
  300.1 7.8 %copy.14 = bf16[4096,1024]{1,0:T(8,128)(2,1)} copy(bf16[4096,1024]{1,0:T(8,128)(2,1)} %get-tuple-element.36) | data formatting | bytes 16777216
  307.9 7.8 %copy.15 = bf16[4096,1024]{1,0:T(8,128)(2,1)} copy(bf16[4096,1024]{1,0:T(8,128)(2,1)} %get-tuple-element.37) | data formatting | bytes 16777216
Async XLA Ops:
  47.6 1.2 copy-start.2
  71.6 1.0 copy-start.1
  287.3 5.8 %copy-start = (f32[4,1024,1024]{2,1,0:T(8,128)S(1)}, f32[4,1024,1024]{2,1,0:T(8,128)}, u32[]{:S(2)}) copy-start(f32[4,1024,1024]{2,1,0:T(8,128)} %get-tuple-element.25.grad_ref) | copy-start | bytes 50331652

commit v3 on v2

v3 whole, which is shorter than its diff:
```python
import functools
import math
import jax
import jax.numpy as jnp
from jax import lax
from jax.experimental import pallas as pl
from jax.experimental.pallas import tpu as pltpu
from jax.sharding import PartitionSpec as P

HEAD_DIM = 128
BLOCK_LEN = 128
BF16 = jnp.bfloat16
F32 = jnp.float32
MESH = pl.DeviceIdType.MESH
CHUNKS = 8
TILE = 256
FIRST = 5
AT0 = (0, 2, 5, 10, 15, 19, 21)
AT = (0, 1, 5, 11, 17, 22, 24)
XAT = (0, 1, 4, 5)
VMEM_LIMIT = 64 * 1024 * 1024 - 1024 * 64


def dot(a, b):
    return lax.dot_general(a, b, (((1,), (0,)), ((), ())), preferred_element_type=F32)


def dot_nt(a, b):
    return lax.dot_general(a, b, (((1,), (1,)), ((), ())), preferred_element_type=F32)


def dot_tn(a, b):
    return lax.dot_general(a, b, (((0,), (0,)), ((), ())), preferred_element_type=F32)


def project_rows(width, x, dy, w_q, w_k, w_v, w_o, z_ref, tot_ref):
    n_groups = z_ref.shape[0]
    for i, value in enumerate((dot(x, w_q), dot(x, w_k), dot(x, w_v), dot_nt(dy, w_o))):
        for g in range(n_groups):
            z_ref[g, :, i * width:(i + 1) * width] = value[:, g * width:(g + 1) * width].astype(BF16)
    per_group = width // HEAD_DIM
    for g in range(n_groups):
        for h in range(per_group):
            q, k, v, do = (z_ref[g, :, i * width + h * HEAD_DIM:i * width + (h + 1) * HEAD_DIM] for i in range(4))
            tot_ref[0, g * per_group + h] += dot_tn(k, v)
            tot_ref[1, g * per_group + h] += dot_tn(q, do)


def project_kernel(width, x_ref, dy_ref, wq_ref, wk_ref, wv_ref, wo_ref, z_ref, tot_ref):
    @pl.when(pl.program_id(0) == 0)
    def _():
        tot_ref[...] = jnp.zeros_like(tot_ref)

    project_rows(width, x_ref[...], dy_ref[...], wq_ref[...], wk_ref[...], wv_ref[...], wo_ref[...], z_ref, tot_ref)


def layer_kernel(att_scale, n_chips, n_groups, width, x_ref, dy_ref, tot_ref, early_hbm, wq_hbm, wk_hbm, wv_hbm, wo_hbm,
                 y_ref, dx_ref, grad_hbm, rows_hbm, late_hbm,
                 state, stage, part, pair, near, own, weights, zin, zout, mats, totals, x_part, x_chip, x_recv, x_half, x_init,
                 stage_sem, weight_sem, tile_sem, local_sem, send_sem, recv_sem, zin_sem, zout_sem, x_send, x_recv_sem):
    step = pl.program_id(0)
    me = lax.axis_index("sp")
    chip, core = me // 2, me % 2
    partner = chip * 2 + (1 - core)
    right_chip, left_chip, far_chip = (chip + 1) % n_chips, (chip + n_chips - 1) % n_chips, (chip + 2) % n_chips
    right, left = right_chip * 2 + core, left_chip * 2 + core
    n_chunks = CHUNKS
    att_steps = n_groups * n_chunks
    chunk = x_ref.shape[0]
    base = 2 * n_chunks
    n_early = early_hbm.shape[0]
    per_group = width // HEAD_DIM
    core_rows = part.shape[1] // 2
    chip_rows = core_rows // n_chips
    half_rows = chip_rows // 2

    def rows_of(owner, half=None, of_core=None):
        base = (core if of_core is None else of_core) * core_rows + owner * chip_rows
        if half is None:
            return pl.ds(pl.multiple_of(base, half_rows), chip_rows)
        return pl.ds(pl.multiple_of(base + half * half_rows, half_rows), half_rows)

    def remote(kind, g, src, dst, target):
        return pltpu.make_async_remote_copy(src, dst, send_sem.at[kind, g], recv_sem.at[kind, g],
                                            device_id={"sp": target}, device_id_type=MESH)

    def message(kind, g):
        if kind == 0:
            other = pl.ds(pl.multiple_of((1 - core) * core_rows, core_rows), core_rows)
            return remote(0, g, part.at[g, other], pair.at[g % 2], partner)
        if kind in (1, 2):
            to, half = ((right, 0), (left, 1))[kind - 1]
            return remote(kind, g, part.at[g, rows_of(far_chip, half)], near.at[g % 2, half], to)
        if kind in (3, 4):
            to, owner = ((right, right_chip), (left, left_chip))[kind - 3]
            return remote(kind, g, part.at[g, rows_of(owner)], own.at[g % 2, kind - 3], to)
        if kind in (5, 6, 7):
            to = (right, left, partner)[kind - 5]
            return remote(kind, g, part.at[g, rows_of(chip)], grad_hbm.at[g, rows_of(chip)], to)
        if kind in (8, 9):
            to, rows = ((right, rows_of(left_chip, 0)), (left, rows_of(right_chip, 1)))[kind - 8]
        else:
            to, rows = partner, rows_of((left_chip, right_chip, far_chip)[kind - 10])
        return remote(kind, g, grad_hbm.at[g, rows], grad_hbm.at[g, rows], to)

    def local(g):
        return pltpu.make_async_copy(part.at[g, rows_of(chip)], grad_hbm.at[g, rows_of(chip)], local_sem.at[g])

    def event(i):
        zeroth = step == FIRST + n_chunks + AT0[i]
        late = step - base - AT[i]
        due = (late >= n_chunks) & (late < att_steps) & (late % n_chunks == 0)
        return zeroth | due, jnp.where(zeroth, 0, late // n_chunks)

    @pl.when(step == 0)
    def _():
        barrier = pltpu.get_barrier_semaphore()
        peers = [partner] + [((chip + o) % n_chips) * 2 + core for o in range(1, n_chips)]
        for peer in peers:
            pl.semaphore_signal(barrier, inc=1, device_id={"sp": peer}, device_id_type=MESH)
        for i, w in enumerate((wq_hbm, wk_hbm, wv_hbm, wo_hbm)):
            pltpu.make_async_copy(w, weights.at[i], weight_sem.at[i]).start()
        totals[0] = tot_ref[...]
        totals[1] = jnp.zeros_like(totals[1])
        pl.semaphore_wait(barrier, len(peers))
        for i, w in enumerate((wq_hbm, wk_hbm, wv_hbm, wo_hbm)):
            pltpu.make_async_copy(w, weights.at[i], weight_sem.at[i]).wait()

    n_half = x_chip.shape[2]
    mine = pl.ds(core * n_half, n_half)
    other = pl.ds((1 - core) * n_half, n_half)

    def x_message(kind, f):
        if kind == 0:
            src, dst, to = totals.at[f], x_part.at[f], partner
        elif kind < n_chips:
            target = (chip + kind) % n_chips
            src, dst, to = x_chip.at[f, jnp.where(target > chip, 0, 1)], x_recv.at[f, kind - 1], target * 2 + core
        else:
            src, dst, to = x_half.at[f, 0], x_half.at[f, 1], partner
        return pltpu.make_async_remote_copy(src, dst, x_send.at[kind, f], x_recv_sem.at[kind, f], device_id={"sp": to}, device_id_type=MESH)

    def x_event(offset):
        late = step - offset
        return (late >= 0) & (late < 4 * n_chunks) & (late % (2 * n_chunks) == 0), late // (2 * n_chunks)

    due, f0 = x_event(XAT[0])

    @pl.when(due)
    def _():
        x_message(0, f0).start()

    due, f1 = x_event(XAT[1])

    @pl.when(due)
    def _():
        x_message(0, f1).wait_recv()
        x_chip[f1] = totals[f1, :, mine] + x_part[f1, :, mine]
        for o in range(1, n_chips):
            x_message(o, f1).start()

    due, f2 = x_event(XAT[2])

    @pl.when(due)
    def _():
        fwd = jnp.zeros(x_recv.shape[2:], F32)
        rev = jnp.zeros(x_recv.shape[2:], F32)
        for o in range(1, n_chips):
            x_message(o, f2).wait_recv()
            early = ((chip + n_chips - o) % n_chips < chip).astype(F32)
            fwd = fwd + early * x_recv[f2, o - 1]
            rev = rev + (1.0 - early) * x_recv[f2, o - 1]
        x_half[f2, 0, 0] = fwd
        x_half[f2, 0, 1] = rev
        x_message(n_chips, f2).start()

    due, f3 = x_event(XAT[3])

    @pl.when(due)
    def _():
        x_message(n_chips, f3).wait_recv()
        is_second = core.astype(F32)
        for slot, heads in ((0, mine), (1, other)):
            x_init[f3, 0, heads] = x_half[f3, slot, 0] + is_second * x_part[f3, 0, heads]
            x_init[f3, 1, heads] = x_half[f3, slot, 1] + (1.0 - is_second) * x_part[f3, 1, heads] + totals[f3, 1, heads]
        for kind in range(n_chips + 1):
            x_message(kind, f3).wait_send()

    due, g0 = event(0)

    @pl.when(due)
    def _():
        message(0, g0).start()

    due, g1 = event(1)

    @pl.when(due)
    def _():
        message(0, g1).wait_recv()
        mine = pl.ds(pl.multiple_of(core * core_rows, core_rows), core_rows)
        part[g1, mine] += pair[g1 % 2]
        message(1, g1).start()
        message(2, g1).start()

    due, g2 = event(2)

    @pl.when(due)
    def _():
        message(1, g2).wait_recv()
        message(2, g2).wait_recv()
        part[g2, rows_of(right_chip, 0)] += near[g2 % 2, 0]
        part[g2, rows_of(left_chip, 1)] += near[g2 % 2, 1]
        message(3, g2).start()
        message(4, g2).start()

    due, g3 = event(3)

    @pl.when(due)
    def _():
        message(3, g3).wait_recv()
        message(4, g3).wait_recv()
        part[g3, rows_of(chip)] += own[g3 % 2, 0] + own[g3 % 2, 1]
        for kind in (5, 6, 7):
            message(kind, g3).start()
        local(g3).start()

    due, g4 = event(4)

    @pl.when(due)
    def _():
        message(5, g4).wait_recv()
        message(6, g4).wait_recv()
        for kind in (8, 9, 10, 11):
            message(kind, g4).start()

    due, g5 = event(5)

    @pl.when(due)
    def _():
        message(8, g5).wait_recv()
        message(9, g5).wait_recv()
        message(12, g5).start()

    due, g6 = event(6)

    @pl.when(due)
    def _():
        for kind in (7, 10, 11, 12):
            message(kind, g6).wait_recv()
        local(g6).wait()
        for kind in range(13):
            message(kind, g6).wait_send()

    def put_stage(s):
        rows = pl.ds(pl.multiple_of((s % n_chunks) * chunk, chunk), chunk)
        return pltpu.make_async_copy(stage.at[s % 2], rows_hbm.at[s // n_chunks, rows], stage_sem.at[s % 2])

    tile_rows = y_ref.shape[0]
    n_tiles = n_chunks * chunk // tile_rows
    per_slab = chunk // tile_rows

    def tile_of(g):
        return g // per_slab, pl.ds(g % per_slab * tile_rows, tile_rows)

    def get_tile(i, act):
        rows = pl.ds(pl.multiple_of(i * tile_rows, tile_rows), tile_rows)
        for g in range(n_groups):
            slab, part_of_slab = tile_of(g)
            act(pltpu.make_async_copy(rows_hbm.at[g, rows], zout.at[i % 2, slab, part_of_slab], tile_sem.at[i % 2, g]))

    def put_z(p):
        rows = pl.ds(pl.multiple_of(p * chunk, chunk), chunk)
        return pltpu.make_async_copy(zout.at[p % 2], late_hbm.at[:, rows], zout_sem.at[p % 2])

    def get_z(t, act):
        g = t // n_chunks
        rows = pl.ds(pl.multiple_of((t % n_chunks) * chunk, chunk), chunk)

        @pl.when(g < n_early)
        def _():
            act(pltpu.make_async_copy(early_hbm.at[jnp.minimum(g, n_early - 1), rows], zin.at[t % 2], zin_sem.at[t % 2]))

        @pl.when(g >= n_early)
        def _():
            act(pltpu.make_async_copy(late_hbm.at[jnp.maximum(g - n_early, 0), rows], zin.at[t % 2], zin_sem.at[t % 2]))

    before = step < FIRST
    p = jnp.where(before, step, step - n_chunks)
    is_project = before | ((step >= FIRST + n_chunks) & (step < base))

    @pl.when((is_project & (p >= 2)) | (step == base) | (step == base + 1))
    def _():
        put_z(p - 2).wait()

    @pl.when(is_project)
    def _():
        late_cols = slice(n_early * width, n_groups * width)
        project_rows(width, x_ref[...], dy_ref[...], weights[0, :, late_cols], weights[1, :, late_cols], weights[2, :, late_cols],
                     weights[3, late_cols, :], zout.at[p % 2], totals.at[1])
        put_z(p).start()

    t = jnp.where(step < base, step - FIRST, step - n_chunks)
    is_attention = ((step >= FIRST) & (step < FIRST + n_chunks)) | ((step >= base) & (step < n_chunks + att_steps))

    @pl.when((step == FIRST - 1) | (is_attention & (t < att_steps - 1)))
    def _():
        get_z(t + 1, lambda copy: copy.start())

    @pl.when((is_attention & (t >= 2)) | (step == n_chunks + att_steps) | (step == n_chunks + att_steps + 1))
    def _():
        put_stage(t - 2).wait()

    @pl.when(is_attention)
    def _():
        g = t // n_chunks

        @pl.when(t % n_chunks == 0)
        def _():
            state[...] = x_init[g // n_early, :, pl.ds((g % n_early) * per_group, per_group)]

        get_z(t, lambda copy: copy.wait())
        slot = t % 2
        row_id = lax.broadcasted_iota(jnp.int32, (BLOCK_LEN, BLOCK_LEN), 0)
        col_id = lax.broadcasted_iota(jnp.int32, (BLOCK_LEN, BLOCK_LEN), 1)
        causal = row_id >= col_id
        n_blocks = chunk // BLOCK_LEN
        pairs = [(h, b) for h in range(per_group) for b in range(n_blocks)]

        def block(i, h, b):
            start = i * width + h * HEAD_DIM
            return zin[slot, b * BLOCK_LEN:(b + 1) * BLOCK_LEN, start:start + HEAD_DIM]

        def beside(left, right):
            return jnp.concatenate([left, right], axis=1)

        def above(top, bottom):
            return jnp.concatenate([top, bottom], axis=0)

        for n, (h, b) in enumerate(pairs):
            q, k, v, do = (block(i, h, b) for i in range(4))
            k_t = k.T
            s16 = state[0, h].astype(BF16)
            state[0, h] += dot(k_t, v)
            r_run = state[1, h] - dot_tn(q, do)
            state[1, h] = r_run
            r16 = r_run.astype(BF16)
            mats[n, 0], mats[n, 1], mats[n, 2], mats[n, 3] = s16, s16.T, r16, r16.T
            a = jnp.where(causal, dot(q, k_t), 0.0).astype(BF16)
            e = jnp.where(causal, dot_nt(do, v), 0.0).astype(BF16)
            mats[n, 4], mats[n, 5], mats[n, 6], mats[n, 7] = a, a.T, e, e.T
        for n, (h, b) in enumerate(pairs):
            q, k, v, do = (block(i, h, b) for i in range(4))
            s16, s16_t, r16, r16_t, a, a_t, e, e_t = (mats[n, i] for i in range(8))
            values = (dot(beside(e, do), above(k, s16_t)), dot(beside(e_t, v), above(q, r16_t)),
                      dot(beside(a_t, k), above(do, r16)), dot(beside(a, q), above(v, s16)))
            for i, value in enumerate(values):
                start = i * width + h * HEAD_DIM
                stage[slot, b * BLOCK_LEN:(b + 1) * BLOCK_LEN, start:start + HEAD_DIM] = (att_scale * value).astype(BF16)
        put_stage(t).start()
        qkv = 3 * width

        @pl.when(t % n_chunks == 0)
        def _():
            part[g, :, :qkv] = dot_tn(x_ref[...], stage[slot, :, :qkv])
            part[g, :, qkv:] = dot_tn(dy_ref[...], stage[slot, :, qkv:])

        @pl.when(t % n_chunks > 0)
        def _():
            part[g, :, :qkv] += dot_tn(x_ref[...], stage[slot, :, :qkv])
            part[g, :, qkv:] += dot_tn(dy_ref[...], stage[slot, :, qkv:])

    tile = step - n_chunks - att_steps - 2

    @pl.when(tile == -1)
    def _():
        get_tile(0, lambda copy: copy.start())

    @pl.when((tile >= 0) & (tile < n_tiles))
    def _():
        @pl.when(tile + 1 < n_tiles)
        def _():
            get_tile(tile + 1, lambda copy: copy.start())

        get_tile(tile, lambda copy: copy.wait())

        def gather(i):
            return jnp.concatenate([zout[(tile % 2,) + tile_of(g) + (slice(i * width, (i + 1) * width),)] for g in range(n_groups)], axis=1)

        dx_ref[...] = (dot_nt(gather(0), weights[0]) + dot_nt(gather(1), weights[1]) + dot_nt(gather(2), weights[2])).astype(BF16)
        y_ref[...] = dot(gather(3), weights[3]).astype(BF16)


def assemble_kernel(n_groups, grad_ref, wq_ref, wk_ref, wv_ref, wo_ref):
    width = grad_ref.shape[2] // 4
    for g in range(n_groups):
        cols = slice(g * width, (g + 1) * width)
        for i, out in enumerate((wq_ref, wk_ref, wv_ref)):
            out[:, cols] = grad_ref[g, :, i * width:(i + 1) * width]
        wo_ref[cols, :] = grad_ref[g, :, 3 * width:].T


def solution(mesh):
    n_seq = mesh.shape["sp"]
    row_spec = P(("dp", "sp"), None)
    grad_spec = P("dp", None)

    def local_layer(tokens, w_q, w_k, w_v, w_o, grad_y):
        n_rows, dim = tokens.shape
        n_heads = dim // HEAD_DIM
        att_scale = 1.0 / math.sqrt(n_rows * n_seq * HEAD_DIM)
        tile = 512
        n_chips = n_seq // 2
        width, chunk, tile_rows = 2 * HEAD_DIM, n_rows // CHUNKS, TILE
        n_groups, n_tiles = dim // width, n_rows // TILE
        n_early = n_groups // 2
        early_cols = n_early * width
        rows_bf16 = jax.ShapeDtypeStruct((n_rows, dim), BF16)
        row_tile = pl.BlockSpec((tile, dim), lambda i: (i, 0))
        some_cols = pl.BlockSpec((dim, early_cols), lambda i: (0, 0), pipeline_mode=pl.Buffered(1))
        some_rows = pl.BlockSpec((early_cols, dim), lambda i: (0, 0), pipeline_mode=pl.Buffered(1))
        state_shape = (2, n_heads // 2, HEAD_DIM, HEAD_DIM)
        whole_state = pl.BlockSpec(state_shape, lambda i: (0, 0, 0, 0))
        half_rows = jax.ShapeDtypeStruct((n_early, n_rows, 4 * width), BF16)
        early, totals = pl.pallas_call(
            functools.partial(project_kernel, width),
            grid=(n_rows // tile,),
            in_specs=[row_tile, row_tile] + [some_cols] * 3 + [some_rows],
            out_specs=[pl.BlockSpec((n_early, tile, 4 * width), lambda i: (0, i, 0)), whole_state],
            out_shape=[half_rows, jax.ShapeDtypeStruct(state_shape, F32)],
            compiler_params=pltpu.CompilerParams(vmem_limit_bytes=VMEM_LIMIT, dimension_semantics=("arbitrary",)),
            name="project",
        )(tokens, grad_y, w_q, w_k, w_v, w_o)

        att_steps = n_groups * CHUNKS
        n_steps = CHUNKS + max(att_steps + 2 + n_tiles, att_steps + AT[6] + 1)

        def tile_index(s):
            return (jnp.clip(s - CHUNKS - att_steps - 2, 0, n_tiles - 1), 0)

        def chunk_index(s):
            late = jnp.minimum(s, CHUNKS + att_steps - 1) % CHUNKS
            return (jnp.where((s >= FIRST) & (s < FIRST + CHUNKS), s - FIRST, late), 0)

        row_chunk = pl.BlockSpec((chunk, dim), chunk_index)
        hbm = pl.BlockSpec(memory_space=pl.ANY)
        out_tile = pl.BlockSpec((tile_rows, dim), tile_index)
        chip_rows = dim // 2 // n_chips
        n_kinds = 13
        head_shape = (n_heads // 4, HEAD_DIM, HEAD_DIM)
        out_y, grad_x, grads, _, _ = pl.pallas_call(
            functools.partial(layer_kernel, att_scale, n_chips, n_groups, width),
            grid=(n_steps,),
            in_specs=[row_chunk] * 2 + [whole_state] + [hbm] * 5,
            out_specs=[out_tile] * 2 + [hbm] * 3,
            out_shape=[rows_bf16] * 2 + [jax.ShapeDtypeStruct((n_groups, dim, 4 * width), F32),
                                         jax.ShapeDtypeStruct((n_groups, n_rows, 4 * width), BF16), half_rows],
            scratch_shapes=[
                pltpu.VMEM((2, width // HEAD_DIM, HEAD_DIM, HEAD_DIM), F32),
                pltpu.VMEM((2, chunk, 4 * width), BF16),
                pltpu.VMEM((n_groups, dim, 4 * width), F32),
                pltpu.VMEM((2, dim // 2, 4 * width), F32),
                pltpu.VMEM((2, 2, chip_rows // 2, 4 * width), F32),
                pltpu.VMEM((2, 2, chip_rows, 4 * width), F32),
                pltpu.VMEM((4, dim, dim), BF16),
                pltpu.VMEM((2, chunk, 4 * width), BF16),
                pltpu.VMEM((2, n_early, chunk, 4 * width), BF16),
                pltpu.VMEM((width // HEAD_DIM * (chunk // BLOCK_LEN), 8, BLOCK_LEN, HEAD_DIM), BF16),
                pltpu.VMEM((2,) + state_shape, F32),
                pltpu.VMEM((2,) + state_shape, F32),
                pltpu.VMEM((2, 2) + head_shape, F32),
                pltpu.VMEM((2, n_chips - 1) + head_shape, F32),
                pltpu.VMEM((2, 2, 2) + head_shape, F32),
                pltpu.VMEM((2,) + state_shape, F32),
                pltpu.SemaphoreType.DMA((2,)),
                pltpu.SemaphoreType.DMA((4,)),
                pltpu.SemaphoreType.DMA((2, n_groups)),
                pltpu.SemaphoreType.DMA((n_groups,)),
                pltpu.SemaphoreType.DMA((n_kinds, n_groups)),
                pltpu.SemaphoreType.DMA((n_kinds, n_groups)),
                pltpu.SemaphoreType.DMA((2,)),
                pltpu.SemaphoreType.DMA((2,)),
                pltpu.SemaphoreType.DMA((n_chips + 1, 2)),
                pltpu.SemaphoreType.DMA((n_chips + 1, 2)),
            ],
            compiler_params=pltpu.CompilerParams(vmem_limit_bytes=VMEM_LIMIT, dimension_semantics=("arbitrary",), collective_id=1, has_side_effects=True),
            name="layer",
        )(tokens, grad_y, totals, early, w_q, w_k, w_v, w_o)

        slab = 128
        grads = pl.pallas_call(
            functools.partial(assemble_kernel, n_groups),
            grid=(dim // slab,),
            in_specs=[pl.BlockSpec((n_groups, slab, 4 * width), lambda i: (0, i, 0))],
            out_specs=[pl.BlockSpec((slab, dim), lambda i: (i, 0))] * 3 + [pl.BlockSpec((dim, slab), lambda i: (0, i))],
            out_shape=[jax.ShapeDtypeStruct((dim, dim), F32)] * 4,
            compiler_params=pltpu.CompilerParams(vmem_limit_bytes=32 * 1024 * 1024, dimension_semantics=("arbitrary",)),
            name="assemble",
        )(grads)
        return (out_y, grad_x) + tuple(grads)

    return jax.shard_map(local_layer, mesh=mesh, in_specs=(row_spec, P(), P(), P(), P(), row_spec),
                         out_specs=(row_spec, row_spec) + (grad_spec,) * 4, check_vma=False)
```

time: 316 us -> 261 us (0.83)
  Pallas kernels: 292 us -> 239 us
    pallas_call x2 -> x1, Pallas kernels: 69.8 us -> 26.9 us  [local_layer(): pl.pallas_call(functools.partial(project_kernel, width), grid=(n_rows //...]
    pallas_call x1, Pallas kernels: 215 us -> 205 us  [local_layer(): pl.pallas_call(functools.partial(layer_kernel, att_scale, n_chips, n_grou...]
    unnamed x8 -> x4, local copies, waits for them, and re-layouts: 23.5 us -> 21.3 us
where the time goes in v3:
time: 261 us
  Pallas kernels  239 us (92%)
  local copies, waits for them, and re-layouts  21.3 us (8%)
    pallas_call x1, Pallas kernels, local_layer(): pl.pallas_call(functools.partial(layer_kernel, att_scale, n_chips, n_grou...  205 us
    pallas_call x1, Pallas kernels, local_layer(): pl.pallas_call(functools.partial(project_kernel, width), grid=(n_rows //...  26.9 us
    unnamed x4, local copies, waits for them, and re-layouts  21.3 us
    pallas_call x1, Pallas kernels, local_layer(): pl.pallas_call(functools.partial(assemble_kernel, n_groups), grid=(dim //...  7.05 us

profile of v3, /device:TPU:81, one launch (start us, length us, event | category | flops | bytes accessed | tf_op | source)
XLA Modules:
  0.0 260.8 jit_solution(877494234607648906)
XLA Ops:
  0.6 26.9 %project.1 = (bf16[2,4096,1024]{2,1,0:T(8,128)(2,1)}, f32[2,4,128,128]{3,2,1,0:T(8,128)}) custom-call(bf16[4096,1024]{1,0:T(8,128)(2,1)} %x_ref.3, bf16[4096,1024]{1,0:T(8,128)(2,1)} %dy_ref.3, bf16[1024,1024]{1,0:T(8,128)(2,1)} %wq_hbm.1, bf16[1024,1024]{1,0:T(8,128)(2,1)} %wk_hbm.1, bf16[1024,1024]{1,0:T(8,128)(2,1)} %wv_hbm.1, bf16[1024,1024]{1,0:T(8,128)(2,1)} %wo_hbm.1), custom_call_target="tpu_custom_call" | custom-call | tf_op jit(solution)/shard_map/project/pallas_call | solution.py:424
  27.5 205.0 %layer.1 = (bf16[4096,1024]{1,0:T(8,128)(2,1)}, bf16[4096,1024]{1,0:T(8,128)(2,1)}, f32[4,1024,1024]{2,1,0:T(8,128)}, bf16[4,4096,1024]{2,1,0:T(8,128)(2,1)}, bf16[2,4096,1024]{2,1,0:T(8,128)(2,1)}) custom-call(bf16[4096,1024]{1,0:T(8,128)(2,1)} %x_ref.3, bf16[4096,1024]{1,0:T(8,128)(2,1)} %dy_ref.3, f32[2,4,128,128]{3,2,1,0:T(8,128)} %get-tuple-element.15.tot_ref, ...), custom_call_target="tpu_custom_call" | custom-call | tf_op jit(solution)/shard_map/layer/pallas_call | solution.py:450
  232.5 0.0 copy-start
  232.5 5.8 %copy-done = f32[4,1024,1024]{2,1,0:T(8,128)S(1)} copy-done((f32[4,1024,1024]{2,1,0:T(8,128)S(1)}, f32[4,1024,1024]{2,1,0:T(8,128)}, u32[]{:S(2)}) %copy-start) | copy-done | bytes 16777240
  238.2 7.0 %assemble.1 = (f32[1024,1024]{1,0:T(8,128)}, f32[1024,1024]{1,0:T(8,128)}, f32[1024,1024]{1,0:T(8,128)}, f32[1024,1024]{1,0:T(8,128)}) custom-call(f32[4,1024,1024]{2,1,0:T(8,128)S(1)} %copy-done), custom_call_target="tpu_custom_call" | custom-call | tf_op jit(solution)/shard_map/assemble/pallas_call | solution.py:490
  245.3 7.8 %copy.14 = bf16[4096,1024]{1,0:T(8,128)(2,1)} copy(bf16[4096,1024]{1,0:T(8,128)(2,1)} %get-tuple-element.30) | data formatting | bytes 16777216
  253.0 7.8 %copy.15 = bf16[4096,1024]{1,0:T(8,128)(2,1)} copy(bf16[4096,1024]{1,0:T(8,128)(2,1)} %get-tuple-element.31) | data formatting | bytes 16777216
Async XLA Ops:
  232.5 5.8 %copy-start = (f32[4,1024,1024]{2,1,0:T(8,128)S(1)}, f32[4,1024,1024]{2,1,0:T(8,128)}, u32[]{:S(2)}) copy-start(f32[4,1024,1024]{2,1,0:T(8,128)} %get-tuple-element.19.grad_ref) | copy-start | bytes 50331652

commit v4 on v3

--- a/solution.py
+++ b/solution.py
@@ -390,7 +390,9 @@
         y_ref[...] = dot(gather(3), weights[3]).astype(BF16)
 
 
-def assemble_kernel(n_groups, grad_ref, wq_ref, wk_ref, wv_ref, wo_ref):
+def assemble_kernel(n_groups, y_in, dx_in, grad_ref, y_ref, dx_ref, wq_ref, wk_ref, wv_ref, wo_ref):
+    y_ref[...] = y_in[...]
+    dx_ref[...] = dx_in[...]
     width = grad_ref.shape[2] // 4
     for g in range(n_groups):
         cols = slice(g * width, (g + 1) * width)
@@ -487,16 +489,17 @@
         )(tokens, grad_y, totals, early, w_q, w_k, w_v, w_o)
 
         slab = 128
-        grads = pl.pallas_call(
+        n_slabs = dim // slab
+        out_rows = pl.BlockSpec((n_rows // n_slabs, dim), lambda i: (i, 0))
+        return pl.pallas_call(
             functools.partial(assemble_kernel, n_groups),
-            grid=(dim // slab,),
-            in_specs=[pl.BlockSpec((n_groups, slab, 4 * width), lambda i: (0, i, 0))],
-            out_specs=[pl.BlockSpec((slab, dim), lambda i: (i, 0))] * 3 + [pl.BlockSpec((dim, slab), lambda i: (0, i))],
-            out_shape=[jax.ShapeDtypeStruct((dim, dim), F32)] * 4,
-            compiler_params=pltpu.CompilerParams(vmem_limit_bytes=32 * 1024 * 1024, dimension_semantics=("arbitrary",)),
+            grid=(n_slabs,),
+            in_specs=[out_rows] * 2 + [pl.BlockSpec((n_groups, slab, 4 * width), lambda i: (0, i, 0))],
+            out_specs=[out_rows] * 2 + [pl.BlockSpec((slab, dim), lambda i: (i, 0))] * 3 + [pl.BlockSpec((dim, slab), lambda i: (0, i))],
+            out_shape=[rows_bf16] * 2 + [jax.ShapeDtypeStruct((dim, dim), F32)] * 4,
+            compiler_params=pltpu.CompilerParams(vmem_limit_bytes=VMEM_LIMIT, dimension_semantics=("arbitrary",)),
             name="assemble",
-        )(grads)
-        return (out_y, grad_x) + tuple(grads)
+        )(out_y, grad_x, grads)
 
     return jax.shard_map(local_layer, mesh=mesh, in_specs=(row_spec, P(), P(), P(), P(), row_spec),
                          out_specs=(row_spec, row_spec) + (grad_spec,) * 4, check_vma=False)

time: 261 us -> 255 us (0.977)
  local copies, waits for them, and re-layouts: 21.3 us -> 0 us
  Pallas kernels: 239 us -> 254 us
    unnamed x4 -> x0, local copies, waits for them, and re-layouts: 21.3 us -> none
    pallas_call x1, Pallas kernels: 7.05 us -> 22.2 us  [local_layer(): pl.pallas_call(functools.partial(assemble_kernel, n_groups), grid=(n_slab...]
where the time goes in v4:
time: 255 us
  Pallas kernels  254 us (100%)
    pallas_call x1, Pallas kernels, local_layer(): pl.pallas_call(functools.partial(layer_kernel, att_scale, n_chips, n_grou...  205 us
    pallas_call x1, Pallas kernels, local_layer(): pl.pallas_call(functools.partial(project_kernel, width), grid=(n_rows //...  26.9 us
    pallas_call x1, Pallas kernels, local_layer(): pl.pallas_call(functools.partial(assemble_kernel, n_groups), grid=(n_slab...  22.2 us

profile of v4, /device:TPU:81, one launch (start us, length us, event | category | flops | bytes accessed | tf_op | source)
XLA Modules:
  0.0 254.6 jit_solution(8590292464187466321)
XLA Ops:
  0.6 26.9 %project.1 = (bf16[2,4096,1024]{2,1,0:T(8,128)(2,1)}, f32[2,4,128,128]{3,2,1,0:T(8,128)}) custom-call(bf16[4096,1024]{1,0:T(8,128)(2,1)} %x_ref.3, bf16[4096,1024]{1,0:T(8,128)(2,1)} %dy_ref.3, bf16[1024,1024]{1,0:T(8,128)(2,1)} %wq_hbm.1, bf16[1024,1024]{1,0:T(8,128)(2,1)} %wk_hbm.1, bf16[1024,1024]{1,0:T(8,128)(2,1)} %wv_hbm.1, bf16[1024,1024]{1,0:T(8,128)(2,1)} %wo_hbm.1), custom_call_target="tpu_custom_call" | custom-call | tf_op jit(solution)/shard_map/project/pallas_call | solution.py:426
  27.5 204.9 %layer.1 = (bf16[4096,1024]{1,0:T(8,128)(2,1)}, bf16[4096,1024]{1,0:T(8,128)(2,1)}, f32[4,1024,1024]{2,1,0:T(8,128)}, bf16[4,4096,1024]{2,1,0:T(8,128)(2,1)}, bf16[2,4096,1024]{2,1,0:T(8,128)(2,1)}) custom-call(bf16[4096,1024]{1,0:T(8,128)(2,1)} %x_ref.3, bf16[4096,1024]{1,0:T(8,128)(2,1)} %dy_ref.3, f32[2,4,128,128]{3,2,1,0:T(8,128)} %get-tuple-element.11.tot_ref, ...), custom_call_target="tpu_custom_call" | custom-call | tf_op jit(solution)/shard_map/layer/pallas_call | solution.py:452
  232.4 22.2 %assemble.1 = (bf16[4096,1024]{1,0:T(8,128)(2,1)}, bf16[4096,1024]{1,0:T(8,128)(2,1)}, f32[1024,1024]{1,0:T(8,128)}, f32[1024,1024]{1,0:T(8,128)}, f32[1024,1024]{1,0:T(8,128)}, /*index=5*/f32[1024,1024]{1,0:T(8,128)}) custom-call(bf16[4096,1024]{1,0:T(8,128)(2,1)} %get-tuple-element.13.y_in, bf16[4096,1024]{1,0:T(8,128)(2,1)} %get-tuple-element.14.dx_in, ...), custom_call_target="tpu_custom_call" | custom-call | tf_op jit(solution)/shard_map/assemble/pallas_call | solution.py:494
